TPU v7x, 32 devices: a whole 2x2x4 slice. The times are simulated.
32 devices in a mesh: cls: 4 (over y, x), dom: 8 (over z, core).
Axes of the slice: x: 2, y: 2, z: 4, core: 2. Of those that a mesh axis runs over, the one named last changes fastest.
Arguments:
- particles: bfloat16 [256, 2, 110592], P(('cls', 'dom')), may hold values from -18 to 18
- labels: int32 [256, 1], P(('cls', 'dom')), may hold values from 0 to 7; in each aligned block of 8 rows (0 to 7, 8 to 15, ...) at most 2 rows name the same one
- wedge_index: int32 [256], P(('cls', 'dom')), may hold values from 0 to 11
- wedge_table: float32 [12, 110592], replicated, may hold values from 0.05 to 1
Outputs:
- class_average: float32 [8, 2, 110592], P('cls', None, 'dom')
- weight_total: float32 [8, 110592], P('cls', 'dom')
Inputs may be any that keep to these rules, and one draw needn't show every extreme that they name: `labels`: among the rows of one device no class appears more than 2 times, and on some devices one class appears exactly 2 times; every class appears on some device.
All inputs are finite; a program needn't handle non-finite values.
Results may differ from a plain program's by a relative error of at most 0.0003.
Values may be sent and summed in bfloat16 or wider, within the bound.
No kernel may reach another device: no remote copies, remote signals or barrier semaphores. Data moves between devices by JAX's collectives and lax.ppermute only.
A program may use at most 128 MiB of HBM per device.

v0:
```python
import functools

import jax
import jax.numpy as jnp
from jax import lax
from jax.experimental import pallas as pl
from jax.experimental.layout import Layout, with_layout_constraint
from jax.experimental.pallas import tpu as pltpu
from jax.sharding import PartitionSpec as P


CLS_GROUP = 2
LANES = 128
SUB = 8
CORES = 2
PARTS = 2
STEPS = 8
CUT = 67
TOP = 32000.0
LEAST = 1e-30
VMEM = pl.BlockSpec(memory_space=pltpu.VMEM)
SMEM = pl.BlockSpec(memory_space=pltpu.SMEM)
HBM = pl.BlockSpec(memory_space=pltpu.HBM)
DMA = pltpu.SemaphoreType.DMA


def up(rows, step=SUB):
    return -(-rows // step) * step


def partner(index, offset, count):
    if count & (count - 1) == 0:
        return index ^ offset
    return (index + offset) % count


def tiles_of(first, rows):
    return (up(rows) - SUB, SUB - 2) if first else (0, 0)


def pack(total, counts, first):
    rows = total.shape[0]
    base, place = tiles_of(first, rows)
    row = lax.broadcasted_iota(jnp.int32, (SUB, LANES), 0)
    edge = total[base : base + SUB]
    edge = jnp.where(row < SUB - 2 if first else row >= SUB - 2, edge, 0.0)
    pieces = [total[:base], edge] if first else [edge, total[SUB:]]
    peak = jnp.full((1, LANES), LEAST, jnp.float32)
    for piece in pieces:
        peak = jnp.maximum(peak, jnp.max(jnp.abs(piece), axis=0, keepdims=True))
    level = jnp.ceil(jnp.log2(peak) * STEPS)
    inverse = TOP * jnp.exp2(level * (-1.0 / STEPS))
    coded = [jnp.round(piece * inverse) for piece in pieces]
    at = 1 if first else 0
    coded[at] = jnp.where(row == place, level, jnp.where(row == place + 1, counts, coded[at]))
    return jnp.concatenate(coded, axis=0).astype(jnp.int32).astype(jnp.int16)


def unpack(coded, first):
    base, place = tiles_of(first, coded.shape[0])
    wide = coded.astype(jnp.int32).astype(jnp.float32)
    at = base + place
    scale = jnp.exp2(wide[at : at + 1] * (1.0 / STEPS)) * (1.0 / TOP)
    return wide * scale, wide[at + 1 : at + 2]


def join(parts, index, first):
    value, counts = unpack(parts[0][index], first)
    for part in parts[1:]:
        more, extra = unpack(part[index], first)
        value, counts = value + more, counts + extra
    return value, counts


def split(cuts, pos, wide, *rest):
    outs, sems = rest[: len(cuts)], rest[-1]
    n_z = outs[0].shape[1]
    copies = []
    for i, (low, high) in enumerate(cuts):
        for z in range(n_z):
            source = wide.at[:, z * CORES + 1 - pos[2], low:high]
            copies.append(pltpu.make_async_copy(source, outs[i].at[:, z], sems.at[i, z]))
    for copy in copies:
        copy.start()
    for copy in copies:
        copy.wait()


def own_sums(pos, meta, table, wide, weights, total, table_buf, wide_buf, sems):
    n_z, p_dev, rows = wide_buf.shape[:3]
    wedges, length = table_buf.shape[1:]
    stride = weights.shape[1] // wedges
    copies = []
    for z in range(n_z):
        shard = z * CORES + pos[2]
        source = table.at[:, pl.ds(pl.multiple_of(shard * length, LANES), length)]
        first = pltpu.make_async_copy(source, table_buf.at[z], sems.at[0, z])
        second = pltpu.make_async_copy(wide.at[:, shard], wide_buf.at[z], sems.at[1, z])
        first.start()
        second.start()
        copies.append((first, second))
    for z in range(n_z):
        for k in range(total.shape[0]):
            total[k, z] = jnp.zeros_like(total[k, z])
    for z in range(n_z):
        copies[z][0].wait()
        for t in range(rows // PARTS):
            for base in range(0, wedges, SUB):
                count = min(SUB, wedges - base)
                tile = table_buf[z, base : base + count, t * LANES : (t + 1) * LANES]
                for c in range(PARTS):
                    weights[z, pl.ds(base * stride + t * PARTS + c, count, stride=stride), :] = tile
        copies[z][1].wait()

        def add(p, carry):
            start = pl.multiple_of(meta[1, p] * stride, SUB)
            total[meta[0, p], z] += weights[z, pl.ds(start, rows), :] * wide_buf[z, p].astype(jnp.float32)
            return carry

        lax.fori_loop(0, p_dev, add, 0)


def chip_sums(n_cls, n_z, by_z, low, stride, pos, own_meta, got_meta, got, weights, begun, *rest):
    outs, total, tally = rest[:-2], rest[-2], rest[-1]
    classes, rows = total.shape[0], total.shape[1]
    held = classes // n_cls
    lane = lax.broadcasted_iota(jnp.int32, (SUB, LANES), 1)
    for k in range(classes):
        tally[k] = jnp.zeros((SUB, LANES), jnp.float32)
    for meta in (own_meta, got_meta):

        def mark(p, carry):
            tally[meta[0, p]] += jnp.where(lane == meta[1, p], 1.0, 0.0)
            return carry

        lax.fori_loop(0, meta.shape[1], mark, 0)
    for j in range(n_z):
        zz = partner(pos[1], j, n_z)
        for k in range(classes):
            total[k] = begun[k, zz, low : low + rows]

        def add(p, carry):
            start = pl.multiple_of(got_meta[1, p] * stride + low, SUB)
            total[got_meta[0, p]] += weights[zz, pl.ds(start, rows), :] * got[p, zz].astype(jnp.float32)
            return carry

        lax.fori_loop(0, got.shape[0], add, 0)
        if by_z:
            for k in range(classes):
                outs[j][k] = pack(total[k], tally[k, 0:1], False)
        else:
            for i in range(n_cls):
                to = partner(pos[0], i, n_cls)
                for h in range(held):
                    k = to * held + h
                    outs[i][h, zz] = pack(total[k], tally[k, 0:1], True)


def sum_cls(n_cls, n_z, pos, *refs):
    parts, outs = refs[:n_cls], refs[n_cls:]
    for j in range(n_z):
        zz = partner(pos[1], j, n_z)
        for h in range(parts[0].shape[0]):
            outs[j][h] = pack(*join(parts, (h, zz), True), True)


def sum_z(n_cls, n_z, pos, *refs):
    parts, outs = refs[:n_z], refs[n_z:]
    held = parts[0].shape[0] // n_cls
    for i in range(n_cls):
        to = partner(pos[0], i, n_cls)
        for h in range(held):
            outs[i][h] = pack(*join(parts, (to * held + h,), False), False)


def finish(n_cls, n_z, cuts, wedges, pos, weights, *refs):
    sides = (refs[:n_z], refs[n_z : n_z + n_cls])
    average, totals, scratch = refs[n_z + n_cls :]
    stride = weights.shape[1] // wedges
    held, rows = average.shape[0], average.shape[1]
    shape = (up(wedges), LANES)
    lane, place = lax.broadcasted_iota(jnp.int32, shape, 1), lax.broadcasted_iota(jnp.int32, shape, 0)
    heads = [join(sides[0], (h,), True) for h in range(held)]
    ends = [join(sides[1], (h,), False)[0] for h in range(held)]
    numbers = [
        jnp.sum(jnp.where(lane == place, counts, 0.0), axis=1, keepdims=True) for _, counts in heads
    ]
    cut = cuts[1][0]
    row = lax.broadcasted_iota(jnp.int32, (SUB, LANES), 0)
    pieces = ((0, cut), (cut, cut + SUB), (cut + SUB, rows))
    for low, high in pieces:
        weight = [jnp.zeros((high - low, LANES), jnp.float32) for _ in range(held)]
        for w in range(wedges):
            one = weights[pos[1], w * stride + low : w * stride + high]
            square = one * one
            for h in range(held):
                weight[h] = weight[h] + numbers[h][w : w + 1] * square
        for h in range(held):
            if low == 0:
                sums = heads[h][0][:cut]
            elif low == cut:
                sums = jnp.where(row < SUB - 2, heads[h][0][cut:], ends[h][:SUB])
            else:
                sums = ends[h][SUB:]
            scratch[h, low:high] = weight[h]
            average[h, low:high] = sums / (weight[h] + 1.0)
    for h in range(held):
        tiles = rows // PARTS
        totals[pl.ds(h, tiles, stride=held), :] = scratch[h, pl.ds(0, tiles, stride=PARTS), :]


def call(body, operands, specs, shapes, scratch=(), flops=1 << 22, limit=16):
    return pl.pallas_call(
        body,
        out_shape=shapes,
        in_specs=specs,
        out_specs=[VMEM] * len(shapes),
        scratch_shapes=list(scratch),
        compiler_params=pltpu.CompilerParams(vmem_limit_bytes=limit * 1024 * 1024),
        cost_estimate=pl.CostEstimate(flops=flops, bytes_accessed=flops, transcendentals=0),
    )(*operands)


def per_device(particles, labels, wedge_index, wedge_table):
    n_cls, n_dom = lax.axis_size("cls"), lax.axis_size("dom")
    n_z = n_dom // CORES
    n_class = n_cls * CLS_GROUP
    p_dev, parts, voxels = particles.shape
    wedges = wedge_table.shape[0]
    tiles = voxels // (n_dom * LANES)
    rows = tiles * parts
    stride = up(rows)
    dom = lax.axis_index("dom")
    pos = jnp.stack([lax.axis_index("cls"), dom // CORES, dom % CORES]).astype(jnp.int32)

    swap = [(d, d ^ 1) for d in range(n_dom)]
    z_moves = [
        [(d, partner(d // CORES, j, n_z) * CORES + d % CORES) for d in range(n_dom)] for j in range(n_z)
    ]
    cls_moves = [[(d, partner(d, i, n_cls)) for d in range(n_cls)] for i in range(n_cls)]

    cut = rows * CUT // 100 // SUB * SUB
    cuts = ((0, cut + SUB), (cut, rows))
    wide = particles.reshape(p_dev, parts, n_dom * tiles, LANES).transpose(0, 2, 1, 3)
    wide = wide.reshape(p_dev, n_dom, rows, LANES)

    def array(dims, kind):
        return jax.ShapeDtypeStruct(dims + (LANES,), kind)

    def held_in_hbm(value):
        return pltpu.with_memory_space_constraint(value, pltpu.HBM)

    meta = jnp.stack([labels[:, 0], wedge_index])
    away = call(
        functools.partial(split, cuts),
        (pos, held_in_hbm(wide)),
        [SMEM, HBM],
        [array((p_dev, n_z, high - low), wide.dtype) for low, high in cuts],
        scratch=[DMA((len(cuts), n_z))],
    )
    got_meta = lax.ppermute(meta, "dom", swap)
    got = [lax.ppermute(a, "dom", swap) for a in away]
    weights, begun = call(
        own_sums,
        (pos, meta, held_in_hbm(wedge_table), held_in_hbm(wide)),
        [SMEM, SMEM, HBM, HBM],
        [array((n_z, wedges * stride), jnp.float32), array((n_class, n_z, rows), jnp.float32)],
        scratch=[
            pltpu.VMEM((n_z, wedges, tiles * LANES), jnp.float32),
            pltpu.VMEM((n_z, p_dev, rows, LANES), wide.dtype),
            DMA((2, n_z)),
        ],
        flops=1 << 24,
    )

    def chip(which, by_z, shapes):
        low, high = cuts[which]
        return call(
            functools.partial(chip_sums, n_cls, n_z, by_z, low, stride),
            (pos, meta, got_meta, got[which], weights, begun),
            [SMEM] * 3 + [VMEM] * 3,
            shapes,
            scratch=[
                pltpu.VMEM((n_class, high - low, LANES), jnp.float32),
                pltpu.VMEM((n_class, SUB, LANES), jnp.float32),
            ],
        )

    def over(axis, moves, arrays):
        moved = list(arrays)
        for i in range(1, len(moves)):
            moved[i] = lax.ppermute(arrays[i], axis, moves[i])
        return moved

    def fold(body, count, arrays, shapes):
        return call(
            functools.partial(body, n_cls, n_z),
            (pos, *arrays),
            [SMEM] + [VMEM] * count,
            shapes,
        )

    size = [high - low for low, high in cuts]
    head = over("cls", cls_moves, chip(0, False, [array((CLS_GROUP, n_z, size[0]), jnp.int16)] * n_cls))
    ends = over("dom", z_moves, chip(1, True, [array((n_class, size[1]), jnp.int16)] * n_z))
    head = fold(sum_cls, n_cls, head, [array((CLS_GROUP, size[0]), jnp.int16)] * n_z)
    head = over("dom", z_moves, head)
    ends = fold(sum_z, n_z, ends, [array((CLS_GROUP, size[1]), jnp.int16)] * n_cls)
    ends = over("cls", cls_moves, ends)
    average, totals = call(
        functools.partial(finish, n_cls, n_z, cuts, wedges),
        (pos, weights, *head, *ends),
        [SMEM] + [VMEM] * (1 + n_z + n_cls),
        [array((CLS_GROUP, rows), jnp.float32), array((tiles * CLS_GROUP,), jnp.float32)],
        scratch=[pltpu.VMEM((CLS_GROUP, rows, LANES), jnp.float32)],
    )
    average = average.reshape(CLS_GROUP, tiles, parts, LANES).transpose(0, 2, 1, 3)
    average = with_layout_constraint(average, Layout(major_to_minor=(0, 2, 1, 3)))
    totals = totals.reshape(tiles, CLS_GROUP, LANES).transpose(1, 0, 2)
    totals = with_layout_constraint(totals, Layout(major_to_minor=(1, 0, 2)))
    return average.reshape(CLS_GROUP, parts, -1), totals.reshape(CLS_GROUP, -1)


def solution(mesh):
    return jax.shard_map(
        per_device,
        mesh=mesh,
        in_specs=(P(("cls", "dom"), None, None), P(("cls", "dom"), None), P(("cls", "dom")), P()),
        out_specs=(P("cls", None, "dom"), P("cls", "dom")),
        check_vma=False,
    )
```

profile of v0, /device:TPU:0, one launch (start us, length us, event | category | flops | bytes accessed | tf_op | source)
XLA Modules:
  0.0 45.0 jit_solution(5741347070135152801)
XLA Ops:
  0.7 0.1 pad_add_fusion.1.pos
  0.7 2.0 %shard_map.60 = (bf16[8,4,152,128]{3,2,1,0:T(8,128)(2,1)S(1)}, bf16[8,4,72,128]{3,2,1,0:T(8,128)(2,1)S(1)}) custom-call(s32[3]{0:T(128)S(1)} %pad_add_fusion.1.pos, bf16[8,8,216,128]{3,2,1,0:T(8,128)(2,1)} %bitcast.20), custom_call_target="tpu_custom_call" | custom-call | flops 4194304 | bytes 4194304 | tf_op jit(solution)/shard_map/pallas_call | solution.py:213
  2.8 0.6 %collective-permute-start.1 = (bf16[8,4,152,128]{3,2,1,0:T(8,128)(2,1)S(1)}, bf16[8,4,152,128]{3,2,1,0:T(8,128)(2,1)S(1)}, u32[]{:S(2)}, u32[]{:S(2)}) collective-permute-start(bf16[8,4,152,128]{3,2,1,0:T(8,128)(2,1)S(1)} %get-tuple-element.25), channel_id=1, source_target_pairs={{0,1},{1,0},{2,3},{3,2},{4,5},{5,4},{6,7},{7,6},{8,9},{9,8},{10,11... | collective-permute-start | bytes 3735560 | tf_op jit(solution)/shard_map/ppermute | solution.py:262
  3.3 0.1 collective-permute-start.8
  3.4 0.5 %collective-permute-start = (s32[2,8]{1,0:T(2,128)S(1)}, s32[2,8]{1,0:T(2,128)S(1)}, u32[]{:S(2)}, u32[]{:S(2)}) collective-permute-start(s32[2,8]{1,0:T(2,128)S(1)} %pad_add_fusion.meta.own_meta), channel_id=1, source_target_pairs={{0,1},{1,0},{2,3},{3,2},{4,5},{5,4},{6,7},{7,6},{8,9},{9,8},{10,11... | collective-permute-start | bytes 200 | tf_op jit(solution)/shard_map/ppermute | solution.py:261
  3.9 3.6 %shard_map.59 = (f32[4,2592,128]{2,1,0:T(8,128)S(1)}, f32[8,4,216,128]{3,2,1,0:T(8,128)S(1)}) custom-call(s32[3]{0:T(128)S(1)} %pad_add_fusion.1.pos, s32[2,8]{1,0:T(2,128)S(1)} %pad_add_fusion.meta.own_meta, f32[12,110592]{1,0:T(8,128)} %table.1, bf16[8,8,216,128]{3,2,1,0:T(8,128)(2,1)} %bitcast.21), custom_call_target="tpu_custom_call" | custom-call | flops 16777216 | bytes 16777216 | tf_op jit(solution)/shard_map/pallas_call | solution.py:213
  7.5 0.0 collective-permute-done.got_meta
  7.5 1.9 %shard_map.61 = (s16[2,4,152,128]{3,2,1,0:T(8,128)(2,1)S(1)}, s16[2,4,152,128]{3,2,1,0:T(8,128)(2,1)S(1)}, s16[2,4,152,128]{3,2,1,0:T(8,128)(2,1)S(1)}, s16[2,4,152,128]{3,2,1,0:T(8,128)(2,1)S(1)}) custom-call(s32[3]{0:T(128)S(1)} %pad_add_fusion.1.pos, s32[2,8]{1,0:T(2,128)S(1)} %pad_add_fusion.meta.own_meta, s32[2,8]{1,0:T(2,128)S(1)} %collective-permute-done.got_meta, ...), custom_call_target="tpu_custom_call" | custom-call | flops 4194304 | bytes 4194304 | tf_op jit(solution)/shard_map/pallas_call | solution.py:213
  9.5 2.6 %collective-permute-start.2 = (s16[2,4,152,128]{3,2,1,0:T(8,128)(2,1)S(1)}, s16[2,4,152,128]{3,2,1,0:T(8,128)(2,1)S(1)}, u32[]{:S(2)}, u32[]{:S(2)}) collective-permute-start(s16[2,4,152,128]{3,2,1,0:T(8,128)(2,1)S(1)} %get-tuple-element.28), channel_id=1, source_target_pairs={{0,8},{8,0},{16,24},{24,16},{1,9},{9,1},{17,25},{25,17},{2,10},{10... | collective-permute-start | bytes 933896 | tf_op jit(solution)/shard_map/ppermute | solution.py:292
  12.1 1.5 %collective-permute-start.3 = (s16[2,4,152,128]{3,2,1,0:T(8,128)(2,1)S(1)}, s16[2,4,152,128]{3,2,1,0:T(8,128)(2,1)S(1)}, u32[]{:S(2)}, u32[]{:S(2)}) collective-permute-start(s16[2,4,152,128]{3,2,1,0:T(8,128)(2,1)S(1)} %get-tuple-element.29), channel_id=1, source_target_pairs={{0,16},{8,24},{16,0},{24,8},{1,17},{9,25},{17,1},{25,9},{2,18},{10... | collective-permute-start | bytes 933896 | tf_op jit(solution)/shard_map/ppermute | solution.py:292
  13.6 0.0 collective-permute-start.4
  13.6 0.0 collective-permute-done.8.got
  13.6 1.5 %shard_map.63 = (s16[8,72,128]{2,1,0:T(8,128)(2,1)S(1)}, s16[8,72,128]{2,1,0:T(8,128)(2,1)S(1)}, s16[8,72,128]{2,1,0:T(8,128)(2,1)S(1)}, s16[8,72,128]{2,1,0:T(8,128)(2,1)S(1)}) custom-call(s32[3]{0:T(128)S(1)} %pad_add_fusion.1.pos, s32[2,8]{1,0:T(2,128)S(1)} %pad_add_fusion.meta.own_meta, s32[2,8]{1,0:T(2,128)S(1)} %collective-permute-done.got_meta, ...), custom_call_target="tpu_custom_call" | custom-call | flops 4194304 | bytes 4194304 | tf_op jit(solution)/shard_map/pallas_call | solution.py:213
  15.2 3.1 %collective-permute-start.10 = (s16[8,72,128]{2,1,0:T(8,128)(2,1)S(1)}, s16[8,72,128]{2,1,0:T(8,128)(2,1)S(1)}, u32[]{:S(2)}, u32[]{:S(2)}) collective-permute-start(s16[8,72,128]{2,1,0:T(8,128)(2,1)S(1)} %get-tuple-element.38), channel_id=1, source_target_pairs={{0,4},{1,5},{2,6},{3,7},{4,0},{5,1},{6,2},{7,3},{8,12},{9,13},{10,... | collective-permute-start | bytes 442376 | tf_op jit(solution)/shard_map/ppermute | solution.py:292
  18.3 1.3 %collective-permute-start.11 = (s16[8,72,128]{2,1,0:T(8,128)(2,1)S(1)}, s16[8,72,128]{2,1,0:T(8,128)(2,1)S(1)}, u32[]{:S(2)}, u32[]{:S(2)}) collective-permute-start(s16[8,72,128]{2,1,0:T(8,128)(2,1)S(1)} %get-tuple-element.39), channel_id=1, source_target_pairs={{0,6},{1,7},{2,4},{3,5},{4,2},{5,3},{6,0},{7,1},{8,14},{9,15},{10,... | collective-permute-start | bytes 442376 | tf_op jit(solution)/shard_map/ppermute | solution.py:292
  19.6 0.7 %collective-permute-done.2.refs_1_ = s16[2,4,152,128]{3,2,1,0:T(8,128)(2,1)S(1)} collective-permute-done((s16[2,4,152,128]{3,2,1,0:T(8,128)(2,1)S(1)}, s16[2,4,152,128]{3,2,1,0:T(8,128)(2,1)S(1)}, u32[]{:S(2)}, u32[]{:S(2)}) %collective-permute-start.2) | collective-permute-done | bytes 311328 | tf_op jit(solution)/shard_map/ppermute | solution.py:292
  20.3 2.1 %collective-permute-start.9 = (s16[8,72,128]{2,1,0:T(8,128)(2,1)S(1)}, s16[8,72,128]{2,1,0:T(8,128)(2,1)S(1)}, u32[]{:S(2)}, u32[]{:S(2)}) collective-permute-start(s16[8,72,128]{2,1,0:T(8,128)(2,1)S(1)} %get-tuple-element.37), channel_id=1, source_target_pairs={{0,2},{1,3},{2,0},{3,1},{4,6},{5,7},{6,4},{7,5},{8,10},{9,11},{10,... | collective-permute-start | bytes 442376 | tf_op jit(solution)/shard_map/ppermute | solution.py:292
  22.4 5.8 %collective-permute-done.3.refs_2_ = s16[2,4,152,128]{3,2,1,0:T(8,128)(2,1)S(1)} collective-permute-done((s16[2,4,152,128]{3,2,1,0:T(8,128)(2,1)S(1)}, s16[2,4,152,128]{3,2,1,0:T(8,128)(2,1)S(1)}, u32[]{:S(2)}, u32[]{:S(2)}) %collective-permute-start.3) | collective-permute-done | bytes 311328 | tf_op jit(solution)/shard_map/ppermute | solution.py:292
  28.2 0.0 collective-permute-done.4.refs_3_
  28.2 1.0 %shard_map.62 = (s16[2,152,128]{2,1,0:T(8,128)(2,1)S(1)}, s16[2,152,128]{2,1,0:T(8,128)(2,1)S(1)}, s16[2,152,128]{2,1,0:T(8,128)(2,1)S(1)}, s16[2,152,128]{2,1,0:T(8,128)(2,1)S(1)}) custom-call(s32[3]{0:T(128)S(1)} %pad_add_fusion.1.pos, s16[2,4,152,128]{3,2,1,0:T(8,128)(2,1)S(1)} %get-tuple-element.27.refs_0_, ...), custom_call_target="tpu_custom_call" | custom-call | flops 4194304 | bytes 4194304 | tf_op jit(solution)/shard_map/pallas_call | solution.py:213
  29.2 1.6 %collective-permute-start.5 = (s16[2,152,128]{2,1,0:T(8,128)(2,1)S(1)}, s16[2,152,128]{2,1,0:T(8,128)(2,1)S(1)}, u32[]{:S(2)}, u32[]{:S(2)}) collective-permute-start(s16[2,152,128]{2,1,0:T(8,128)(2,1)S(1)} %get-tuple-element.32), channel_id=1, source_target_pairs={{0,2},{1,3},{2,0},{3,1},{4,6},{5,7},{6,4},{7,5},{8,10},{9,11},{10,... | collective-permute-start | bytes 233480 | tf_op jit(solution)/shard_map/ppermute | solution.py:292
  30.8 2.6 %collective-permute-start.6 = (s16[2,152,128]{2,1,0:T(8,128)(2,1)S(1)}, s16[2,152,128]{2,1,0:T(8,128)(2,1)S(1)}, u32[]{:S(2)}, u32[]{:S(2)}) collective-permute-start(s16[2,152,128]{2,1,0:T(8,128)(2,1)S(1)} %get-tuple-element.33), channel_id=1, source_target_pairs={{0,4},{1,5},{2,6},{3,7},{4,0},{5,1},{6,2},{7,3},{8,12},{9,13},{10,... | collective-permute-start | bytes 233480 | tf_op jit(solution)/shard_map/ppermute | solution.py:292
  33.4 0.2 collective-permute-start.7
  33.7 0.0 collective-permute-done.9.refs_1_
  33.7 0.8 %shard_map.64 = (s16[2,72,128]{2,1,0:T(8,128)(2,1)S(1)}, s16[2,72,128]{2,1,0:T(8,128)(2,1)S(1)}, s16[2,72,128]{2,1,0:T(8,128)(2,1)S(1)}, s16[2,72,128]{2,1,0:T(8,128)(2,1)S(1)}) custom-call(s32[3]{0:T(128)S(1)} %pad_add_fusion.1.pos, s16[8,72,128]{2,1,0:T(8,128)(2,1)S(1)} %get-tuple-element.36.refs_0_, ...), custom_call_target="tpu_custom_call" | custom-call | flops 4194304 | bytes 4194304 | tf_op jit(solution)/shard_map/pallas_call | solution.py:213
  34.5 1.3 %collective-permute-start.12 = (s16[2,72,128]{2,1,0:T(8,128)(2,1)S(1)}, s16[2,72,128]{2,1,0:T(8,128)(2,1)S(1)}, u32[]{:S(2)}, u32[]{:S(2)}) collective-permute-start(s16[2,72,128]{2,1,0:T(8,128)(2,1)S(1)} %get-tuple-element.41), channel_id=1, source_target_pairs={{0,8},{8,0},{16,24},{24,16},{1,9},{9,1},{17,25},{25,17},{2,10},{10... | collective-permute-start | bytes 110600 | tf_op jit(solution)/shard_map/ppermute | solution.py:292
  35.8 0.8 %collective-permute-start.13 = (s16[2,72,128]{2,1,0:T(8,128)(2,1)S(1)}, s16[2,72,128]{2,1,0:T(8,128)(2,1)S(1)}, u32[]{:S(2)}, u32[]{:S(2)}) collective-permute-start(s16[2,72,128]{2,1,0:T(8,128)(2,1)S(1)} %get-tuple-element.42), channel_id=1, source_target_pairs={{0,16},{8,24},{16,0},{24,8},{1,17},{9,25},{17,1},{25,9},{2,18},{10... | collective-permute-start | bytes 110600 | tf_op jit(solution)/shard_map/ppermute | solution.py:292
  36.6 1.9 %collective-permute-done.12.refs_5_ = s16[2,72,128]{2,1,0:T(8,128)(2,1)S(1)} collective-permute-done((s16[2,72,128]{2,1,0:T(8,128)(2,1)S(1)}, s16[2,72,128]{2,1,0:T(8,128)(2,1)S(1)}, u32[]{:S(2)}, u32[]{:S(2)}) %collective-permute-start.12) | collective-permute-done | bytes 36896 | tf_op jit(solution)/shard_map/ppermute | solution.py:292
  38.5 1.5 %collective-permute-start.14 = (s16[2,72,128]{2,1,0:T(8,128)(2,1)S(1)}, s16[2,72,128]{2,1,0:T(8,128)(2,1)S(1)}, u32[]{:S(2)}, u32[]{:S(2)}) collective-permute-start(s16[2,72,128]{2,1,0:T(8,128)(2,1)S(1)} %get-tuple-element.43), channel_id=1, source_target_pairs={{0,24},{8,16},{16,8},{24,0},{1,25},{9,17},{17,9},{25,1},{2,26},{10... | collective-permute-start | bytes 110600 | tf_op jit(solution)/shard_map/ppermute | solution.py:292
  40.0 3.4 %collective-permute-done.14.refs_7_ = s16[2,72,128]{2,1,0:T(8,128)(2,1)S(1)} collective-permute-done((s16[2,72,128]{2,1,0:T(8,128)(2,1)S(1)}, s16[2,72,128]{2,1,0:T(8,128)(2,1)S(1)}, u32[]{:S(2)}, u32[]{:S(2)}) %collective-permute-start.14) | collective-permute-done | bytes 36896 | tf_op jit(solution)/shard_map/ppermute | solution.py:292
  43.3 0.0 collective-permute-done.7.refs_3_
  43.3 1.7 %shard_map.65 = (f32[2,216,128]{2,1,0:T(8,128)}, f32[216,128]{1,0:T(8,128)}) custom-call(s32[3]{0:T(128)S(1)} %pad_add_fusion.1.pos, f32[4,2592,128]{2,1,0:T(8,128)S(1)} %get-tuple-element.24.weights, s16[2,152,128]{2,1,0:T(8,128)(2,1)S(1)} %get-tuple-element.31.refs_0_, s16[2,152,128]{2,1,0:T(8,128)(2,1)S(1)} %collective-permute-done.5.refs_1_, ...), custom_call_target="tpu_custom_call" | custom-call | flops 4194304 | bytes 4194304 | tf_op jit(solution)/shard_map/pallas_call | solution.py:213
  (11 shorter events, 0.0 us)
Async XLA Ops:
  0.6 2.8 %copy-start.1 = (s32[8,1]{0,1:T(1,128)S(1)}, s32[8,1]{0,1:T(1,128)}, u32[]{:S(2)}) copy-start(s32[8,1]{0,1:T(1,128)} %param.5) | copy-start | bytes 100
  0.6 2.8 %copy-start = (s32[8]{0:T(128)S(1)}, s32[8]{0:T(128)}, u32[]{:S(2)}) copy-start(s32[8]{0:T(128)} %param.6) | copy-start | bytes 100
  2.8 4.7 %collective-permute-start.1 = (bf16[8,4,152,128]{3,2,1,0:T(8,128)(2,1)S(1)}, bf16[8,4,152,128]{3,2,1,0:T(8,128)(2,1)S(1)}, u32[]{:S(2)}, u32[]{:S(2)}) collective-permute-start(bf16[8,4,152,128]{3,2,1,0:T(8,128)(2,1)S(1)} %get-tuple-element.25), channel_id=1, source_target_pairs={{0,1},{1,0},{2,3},{3,2},{4,5},{5,4},{6,7},{7,6},{8,9},{9,8},{10,11... | collective-permute-start | bytes 3735560 | tf_op jit(solution)/shard_map/ppermute | solution.py:262
  3.3 10.3 %collective-permute-start.8 = (bf16[8,4,72,128]{3,2,1,0:T(8,128)(2,1)S(1)}, bf16[8,4,72,128]{3,2,1,0:T(8,128)(2,1)S(1)}, u32[]{:S(2)}, u32[]{:S(2)}) collective-permute-start(bf16[8,4,72,128]{3,2,1,0:T(8,128)(2,1)S(1)} %get-tuple-element.35), channel_id=1, source_target_pairs={{0,1},{1,0},{2,3},{3,2},{4,5},{5,4},{6,7},{7,6},{8,9},{9,8},{10,11... | collective-permute-start | bytes 1769480 | tf_op jit(solution)/shard_map/ppermute | solution.py:262
  3.4 4.1 %collective-permute-start = (s32[2,8]{1,0:T(2,128)S(1)}, s32[2,8]{1,0:T(2,128)S(1)}, u32[]{:S(2)}, u32[]{:S(2)}) collective-permute-start(s32[2,8]{1,0:T(2,128)S(1)} %pad_add_fusion.meta.own_meta), channel_id=1, source_target_pairs={{0,1},{1,0},{2,3},{3,2},{4,5},{5,4},{6,7},{7,6},{8,9},{9,8},{10,11... | collective-permute-start | bytes 200 | tf_op jit(solution)/shard_map/ppermute | solution.py:261
  9.5 10.8 %collective-permute-start.2 = (s16[2,4,152,128]{3,2,1,0:T(8,128)(2,1)S(1)}, s16[2,4,152,128]{3,2,1,0:T(8,128)(2,1)S(1)}, u32[]{:S(2)}, u32[]{:S(2)}) collective-permute-start(s16[2,4,152,128]{3,2,1,0:T(8,128)(2,1)S(1)} %get-tuple-element.28), channel_id=1, source_target_pairs={{0,8},{8,0},{16,24},{24,16},{1,9},{9,1},{17,25},{25,17},{2,10},{10... | collective-permute-start | bytes 933896 | tf_op jit(solution)/shard_map/ppermute | solution.py:292
  12.1 16.1 %collective-permute-start.3 = (s16[2,4,152,128]{3,2,1,0:T(8,128)(2,1)S(1)}, s16[2,4,152,128]{3,2,1,0:T(8,128)(2,1)S(1)}, u32[]{:S(2)}, u32[]{:S(2)}) collective-permute-start(s16[2,4,152,128]{3,2,1,0:T(8,128)(2,1)S(1)} %get-tuple-element.29), channel_id=1, source_target_pairs={{0,16},{8,24},{16,0},{24,8},{1,17},{9,25},{17,1},{25,9},{2,18},{10... | collective-permute-start | bytes 933896 | tf_op jit(solution)/shard_map/ppermute | solution.py:292
  13.6 14.6 %collective-permute-start.4 = (s16[2,4,152,128]{3,2,1,0:T(8,128)(2,1)S(1)}, s16[2,4,152,128]{3,2,1,0:T(8,128)(2,1)S(1)}, u32[]{:S(2)}, u32[]{:S(2)}) collective-permute-start(s16[2,4,152,128]{3,2,1,0:T(8,128)(2,1)S(1)} %get-tuple-element.30), channel_id=1, source_target_pairs={{0,24},{8,16},{16,8},{24,0},{1,25},{9,17},{17,9},{25,1},{2,26},{10... | collective-permute-start | bytes 933896 | tf_op jit(solution)/shard_map/ppermute | solution.py:292
  15.2 18.3 %collective-permute-start.10 = (s16[8,72,128]{2,1,0:T(8,128)(2,1)S(1)}, s16[8,72,128]{2,1,0:T(8,128)(2,1)S(1)}, u32[]{:S(2)}, u32[]{:S(2)}) collective-permute-start(s16[8,72,128]{2,1,0:T(8,128)(2,1)S(1)} %get-tuple-element.38), channel_id=1, source_target_pairs={{0,4},{1,5},{2,6},{3,7},{4,0},{5,1},{6,2},{7,3},{8,12},{9,13},{10,... | collective-permute-start | bytes 442376 | tf_op jit(solution)/shard_map/ppermute | solution.py:292
  18.3 15.4 %collective-permute-start.11 = (s16[8,72,128]{2,1,0:T(8,128)(2,1)S(1)}, s16[8,72,128]{2,1,0:T(8,128)(2,1)S(1)}, u32[]{:S(2)}, u32[]{:S(2)}) collective-permute-start(s16[8,72,128]{2,1,0:T(8,128)(2,1)S(1)} %get-tuple-element.39), channel_id=1, source_target_pairs={{0,6},{1,7},{2,4},{3,5},{4,2},{5,3},{6,0},{7,1},{8,14},{9,15},{10,... | collective-permute-start | bytes 442376 | tf_op jit(solution)/shard_map/ppermute | solution.py:292
  20.3 13.3 %collective-permute-start.9 = (s16[8,72,128]{2,1,0:T(8,128)(2,1)S(1)}, s16[8,72,128]{2,1,0:T(8,128)(2,1)S(1)}, u32[]{:S(2)}, u32[]{:S(2)}) collective-permute-start(s16[8,72,128]{2,1,0:T(8,128)(2,1)S(1)} %get-tuple-element.37), channel_id=1, source_target_pairs={{0,2},{1,3},{2,0},{3,1},{4,6},{5,7},{6,4},{7,5},{8,10},{9,11},{10,... | collective-permute-start | bytes 442376 | tf_op jit(solution)/shard_map/ppermute | solution.py:292
  29.2 14.1 %collective-permute-start.5 = (s16[2,152,128]{2,1,0:T(8,128)(2,1)S(1)}, s16[2,152,128]{2,1,0:T(8,128)(2,1)S(1)}, u32[]{:S(2)}, u32[]{:S(2)}) collective-permute-start(s16[2,152,128]{2,1,0:T(8,128)(2,1)S(1)} %get-tuple-element.32), channel_id=1, source_target_pairs={{0,2},{1,3},{2,0},{3,1},{4,6},{5,7},{6,4},{7,5},{8,10},{9,11},{10,... | collective-permute-start | bytes 233480 | tf_op jit(solution)/shard_map/ppermute | solution.py:292
  30.8 12.5 %collective-permute-start.6 = (s16[2,152,128]{2,1,0:T(8,128)(2,1)S(1)}, s16[2,152,128]{2,1,0:T(8,128)(2,1)S(1)}, u32[]{:S(2)}, u32[]{:S(2)}) collective-permute-start(s16[2,152,128]{2,1,0:T(8,128)(2,1)S(1)} %get-tuple-element.33), channel_id=1, source_target_pairs={{0,4},{1,5},{2,6},{3,7},{4,0},{5,1},{6,2},{7,3},{8,12},{9,13},{10,... | collective-permute-start | bytes 233480 | tf_op jit(solution)/shard_map/ppermute | solution.py:292
  33.4 9.9 %collective-permute-start.7 = (s16[2,152,128]{2,1,0:T(8,128)(2,1)S(1)}, s16[2,152,128]{2,1,0:T(8,128)(2,1)S(1)}, u32[]{:S(2)}, u32[]{:S(2)}) collective-permute-start(s16[2,152,128]{2,1,0:T(8,128)(2,1)S(1)} %get-tuple-element.34), channel_id=1, source_target_pairs={{0,6},{1,7},{2,4},{3,5},{4,2},{5,3},{6,0},{7,1},{8,14},{9,15},{10,... | collective-permute-start | bytes 233480 | tf_op jit(solution)/shard_map/ppermute | solution.py:292
  34.5 4.0 %collective-permute-start.12 = (s16[2,72,128]{2,1,0:T(8,128)(2,1)S(1)}, s16[2,72,128]{2,1,0:T(8,128)(2,1)S(1)}, u32[]{:S(2)}, u32[]{:S(2)}) collective-permute-start(s16[2,72,128]{2,1,0:T(8,128)(2,1)S(1)} %get-tuple-element.41), channel_id=1, source_target_pairs={{0,8},{8,0},{16,24},{24,16},{1,9},{9,1},{17,25},{25,17},{2,10},{10... | collective-permute-start | bytes 110600 | tf_op jit(solution)/shard_map/ppermute | solution.py:292
  35.8 4.2 %collective-permute-start.13 = (s16[2,72,128]{2,1,0:T(8,128)(2,1)S(1)}, s16[2,72,128]{2,1,0:T(8,128)(2,1)S(1)}, u32[]{:S(2)}, u32[]{:S(2)}) collective-permute-start(s16[2,72,128]{2,1,0:T(8,128)(2,1)S(1)} %get-tuple-element.42), channel_id=1, source_target_pairs={{0,16},{8,24},{16,0},{24,8},{1,17},{9,25},{17,1},{25,9},{2,18},{10... | collective-permute-start | bytes 110600 | tf_op jit(solution)/shard_map/ppermute | solution.py:292
  38.5 4.9 %collective-permute-start.14 = (s16[2,72,128]{2,1,0:T(8,128)(2,1)S(1)}, s16[2,72,128]{2,1,0:T(8,128)(2,1)S(1)}, u32[]{:S(2)}, u32[]{:S(2)}) collective-permute-start(s16[2,72,128]{2,1,0:T(8,128)(2,1)S(1)} %get-tuple-element.43), channel_id=1, source_target_pairs={{0,24},{8,16},{16,8},{24,0},{1,25},{9,17},{17,9},{25,1},{2,26},{10... | collective-permute-start | bytes 110600 | tf_op jit(solution)/shard_map/ppermute | solution.py:292
where the time goes:
time: 45.2 us; the launch traced here: 45 us
  starting transfers between devices  19.9 us (44%)
  Pallas kernels  12.5 us (28%)
  waiting for transfers between devices  11.8 us (26%)
  between operations  0.74 us (2%)
    ppermute x12, starting transfers between devices, over(): moved[i] = lax.ppermute(arrays[i], axis, moves[i])  18.8 us
    pallas_call x7, Pallas kernels, call(): pl.pallas_call(body, out_shape=shapes, in_specs=specs, out_specs=[VMEM] *...  12.5 us
    ppermute x12, waiting for transfers between devices, over(): moved[i] = lax.ppermute(arrays[i], axis, moves[i])  11.8 us
  transfers between devices with their start and end apart: 15, of which 4 were waited for; matrix products, arithmetic and copies ran while one was open for 0% of the time, Pallas kernels for 20%

commit v1 on v0

--- a/solution.py
+++ b/solution.py
@@ -19,13 +19,22 @@
 TOP = 32000.0
 LEAST = 1e-30
 VMEM = pl.BlockSpec(memory_space=pltpu.VMEM)
-SMEM = pl.BlockSpec(memory_space=pltpu.SMEM)
 HBM = pl.BlockSpec(memory_space=pltpu.HBM)
 DMA = pltpu.SemaphoreType.DMA
 
 
 def up(rows, step=SUB):
     return -(-rows // step) * step
+
+
+def position():
+    dom = lax.axis_index("dom")
+    return lax.axis_index("cls"), lax.div(dom, CORES), lax.rem(dom, CORES)
+
+
+def numbers_of(meta):
+    found = meta[...]
+    return [(found[0, p], found[1, p]) for p in range(meta.shape[1])]
 
 
 def partner(index, offset, count):
@@ -72,7 +81,8 @@
     return value, counts
 
 
-def split(cuts, pos, wide, *rest):
+def split(cuts, wide, *rest):
+    pos = position()
     outs, sems = rest[: len(cuts)], rest[-1]
     n_z = outs[0].shape[1]
     copies = []
@@ -86,8 +96,9 @@
         copy.wait()
 
 
-def own_sums(pos, meta, table, wide, weights, total, table_buf, wide_buf, sems):
-    n_z, p_dev, rows = wide_buf.shape[:3]
+def own_sums(meta, table, wide, weights, total, tally, table_buf, wide_buf, sems):
+    pos = position()
+    n_z, _, rows = wide_buf.shape[:3]
     wedges, length = table_buf.shape[1:]
     stride = weights.shape[1] // wedges
     copies = []
@@ -99,9 +110,14 @@
         first.start()
         second.start()
         copies.append((first, second))
+    named = numbers_of(meta)
     for z in range(n_z):
         for k in range(total.shape[0]):
             total[k, z] = jnp.zeros_like(total[k, z])
+    tally[...] = jnp.zeros_like(tally)
+    lane = lax.broadcasted_iota(jnp.int32, (SUB, LANES), 1)
+    for k, w in named:
+        tally[k] += jnp.where(lane == w, 1.0, 0.0)
     for z in range(n_z):
         copies[z][0].wait()
         for t in range(rows // PARTS):
@@ -112,39 +128,28 @@
                     weights[z, pl.ds(base * stride + t * PARTS + c, count, stride=stride), :] = tile
         copies[z][1].wait()
 
-        def add(p, carry):
-            start = pl.multiple_of(meta[1, p] * stride, SUB)
-            total[meta[0, p], z] += weights[z, pl.ds(start, rows), :] * wide_buf[z, p].astype(jnp.float32)
-            return carry
-
-        lax.fori_loop(0, p_dev, add, 0)
-
-
-def chip_sums(n_cls, n_z, by_z, low, stride, pos, own_meta, got_meta, got, weights, begun, *rest):
+        for p, (k, w) in enumerate(named):
+            start = pl.multiple_of(w * stride, SUB)
+            total[k, z] += weights[z, pl.ds(start, rows), :] * wide_buf[z, p].astype(jnp.float32)
+
+
+def chip_sums(n_cls, n_z, by_z, low, stride, got_meta, got, weights, begun, own_tally, *rest):
+    pos = position()
     outs, total, tally = rest[:-2], rest[-2], rest[-1]
     classes, rows = total.shape[0], total.shape[1]
     held = classes // n_cls
+    named = numbers_of(got_meta)
     lane = lax.broadcasted_iota(jnp.int32, (SUB, LANES), 1)
-    for k in range(classes):
-        tally[k] = jnp.zeros((SUB, LANES), jnp.float32)
-    for meta in (own_meta, got_meta):
-
-        def mark(p, carry):
-            tally[meta[0, p]] += jnp.where(lane == meta[1, p], 1.0, 0.0)
-            return carry
-
-        lax.fori_loop(0, meta.shape[1], mark, 0)
+    tally[...] = own_tally[...]
+    for k, w in named:
+        tally[k] += jnp.where(lane == w, 1.0, 0.0)
     for j in range(n_z):
         zz = partner(pos[1], j, n_z)
         for k in range(classes):
             total[k] = begun[k, zz, low : low + rows]
-
-        def add(p, carry):
-            start = pl.multiple_of(got_meta[1, p] * stride + low, SUB)
-            total[got_meta[0, p]] += weights[zz, pl.ds(start, rows), :] * got[p, zz].astype(jnp.float32)
-            return carry
-
-        lax.fori_loop(0, got.shape[0], add, 0)
+        for p, (k, w) in enumerate(named):
+            start = pl.multiple_of(w * stride + low, SUB)
+            total[k] += weights[zz, pl.ds(start, rows), :] * got[p, zz].astype(jnp.float32)
         if by_z:
             for k in range(classes):
                 outs[j][k] = pack(total[k], tally[k, 0:1], False)
@@ -156,7 +161,8 @@
                     outs[i][h, zz] = pack(total[k], tally[k, 0:1], True)
 
 
-def sum_cls(n_cls, n_z, pos, *refs):
+def sum_cls(n_cls, n_z, *refs):
+    pos = position()
     parts, outs = refs[:n_cls], refs[n_cls:]
     for j in range(n_z):
         zz = partner(pos[1], j, n_z)
@@ -164,7 +170,8 @@
             outs[j][h] = pack(*join(parts, (h, zz), True), True)
 
 
-def sum_z(n_cls, n_z, pos, *refs):
+def sum_z(n_cls, n_z, *refs):
+    pos = position()
     parts, outs = refs[:n_z], refs[n_z:]
     held = parts[0].shape[0] // n_cls
     for i in range(n_cls):
@@ -173,7 +180,8 @@
             outs[i][h] = pack(*join(parts, (to * held + h,), False), False)
 
 
-def finish(n_cls, n_z, cuts, wedges, pos, weights, *refs):
+def finish(n_cls, n_z, cuts, wedges, weights, *refs):
+    pos = position()
     sides = (refs[:n_z], refs[n_z : n_z + n_cls])
     average, totals, scratch = refs[n_z + n_cls :]
     stride = weights.shape[1] // wedges
@@ -230,8 +238,6 @@
     tiles = voxels // (n_dom * LANES)
     rows = tiles * parts
     stride = up(rows)
-    dom = lax.axis_index("dom")
-    pos = jnp.stack([lax.axis_index("cls"), dom // CORES, dom % CORES]).astype(jnp.int32)
 
     swap = [(d, d ^ 1) for d in range(n_dom)]
     z_moves = [
@@ -253,18 +259,18 @@
     meta = jnp.stack([labels[:, 0], wedge_index])
     away = call(
         functools.partial(split, cuts),
-        (pos, held_in_hbm(wide)),
-        [SMEM, HBM],
+        (held_in_hbm(wide),),
+        [HBM],
         [array((p_dev, n_z, high - low), wide.dtype) for low, high in cuts],
         scratch=[DMA((len(cuts), n_z))],
     )
     got_meta = lax.ppermute(meta, "dom", swap)
     got = [lax.ppermute(a, "dom", swap) for a in away]
-    weights, begun = call(
+    weights, begun, tally = call(
         own_sums,
-        (pos, meta, held_in_hbm(wedge_table), held_in_hbm(wide)),
-        [SMEM, SMEM, HBM, HBM],
-        [array((n_z, wedges * stride), jnp.float32), array((n_class, n_z, rows), jnp.float32)],
+        (meta, held_in_hbm(wedge_table), held_in_hbm(wide)),
+        [VMEM, HBM, HBM],
+        [array((n_z, wedges * stride), jnp.float32), array((n_class, n_z, rows), jnp.float32), array((n_class, SUB), jnp.float32)],
         scratch=[
             pltpu.VMEM((n_z, wedges, tiles * LANES), jnp.float32),
             pltpu.VMEM((n_z, p_dev, rows, LANES), wide.dtype),
@@ -277,8 +283,8 @@
         low, high = cuts[which]
         return call(
             functools.partial(chip_sums, n_cls, n_z, by_z, low, stride),
-            (pos, meta, got_meta, got[which], weights, begun),
-            [SMEM] * 3 + [VMEM] * 3,
+            (got_meta, got[which], weights, begun, tally),
+            [VMEM] * 5,
             shapes,
             scratch=[
                 pltpu.VMEM((n_class, high - low, LANES), jnp.float32),
@@ -295,8 +301,8 @@
     def fold(body, count, arrays, shapes):
         return call(
             functools.partial(body, n_cls, n_z),
-            (pos, *arrays),
-            [SMEM] + [VMEM] * count,
+            tuple(arrays),
+            [VMEM] * count,
             shapes,
         )
 
@@ -309,8 +315,8 @@
     ends = over("cls", cls_moves, ends)
     average, totals = call(
         functools.partial(finish, n_cls, n_z, cuts, wedges),
-        (pos, weights, *head, *ends),
-        [SMEM] + [VMEM] * (1 + n_z + n_cls),
+        (weights, *head, *ends),
+        [VMEM] * (1 + n_z + n_cls),
         [array((CLS_GROUP, rows), jnp.float32), array((tiles * CLS_GROUP,), jnp.float32)],
         scratch=[pltpu.VMEM((CLS_GROUP, rows, LANES), jnp.float32)],
     )

time: 45.2 us -> 41.7 us (0.923)
  Pallas kernels: 12.5 us -> 8.3 us
  waiting for transfers between devices: 11.8 us -> 12.5 us
    pallas_call x7, Pallas kernels: 12.5 us -> 8.3 us  [call(): pl.pallas_call(body, out_shape=shapes, in_specs=specs, out_specs=[VMEM] *...]
    ppermute x12, waiting for transfers between devices: 11.8 us -> 12.5 us  [over(): moved[i] = lax.ppermute(arrays[i], axis, moves[i])]
  transfers between devices with their start and end apart: 15 -> 15, of which waited for: 4 -> 4; matrix products, arithmetic and copies ran while one was open for 0% -> 0% of each run, Pallas kernels for 20% -> 14%
where the time goes in v1:
time: 41.7 us; the launch traced here: 41.6 us
  starting transfers between devices  20.1 us (48%)
  waiting for transfers between devices  12.5 us (30%)
  Pallas kernels  8.3 us (20%)
  between operations  0.72 us (2%)
    ppermute x12, starting transfers between devices, over(): moved[i] = lax.ppermute(arrays[i], axis, moves[i])  18.9 us
    ppermute x12, waiting for transfers between devices, over(): moved[i] = lax.ppermute(arrays[i], axis, moves[i])  12.5 us
    pallas_call x7, Pallas kernels, call(): pl.pallas_call(body, out_shape=shapes, in_specs=specs, out_specs=[VMEM] *...  8.3 us
  transfers between devices with their start and end apart: 15, of which 4 were waited for; matrix products, arithmetic and copies ran while one was open for 0% of the time, Pallas kernels for 14%

profile of v1, /device:TPU:0, one launch (start us, length us, event | category | flops | bytes accessed | tf_op | source)
XLA Modules:
  0.0 41.6 jit_solution(2777037521949921113)
XLA Ops:
  0.6 1.5 %shard_map.60 = (bf16[8,4,152,128]{3,2,1,0:T(8,128)(2,1)S(1)}, bf16[8,4,72,128]{3,2,1,0:T(8,128)(2,1)S(1)}) custom-call(bf16[8,8,216,128]{3,2,1,0:T(8,128)(2,1)} %bitcast.17), custom_call_target="tpu_custom_call" | custom-call | flops 4194304 | bytes 4194304 | tf_op jit(solution)/shard_map/pallas_call | solution.py:221
  2.2 0.6 %collective-permute-start.1 = (bf16[8,4,152,128]{3,2,1,0:T(8,128)(2,1)S(1)}, bf16[8,4,152,128]{3,2,1,0:T(8,128)(2,1)S(1)}, u32[]{:S(2)}, u32[]{:S(2)}) collective-permute-start(bf16[8,4,152,128]{3,2,1,0:T(8,128)(2,1)S(1)} %get-tuple-element.26), channel_id=1, source_target_pairs={{0,1},{1,0},{2,3},{3,2},{4,5},{5,4},{6,7},{7,6},{8,9},{9,8},{10,11... | collective-permute-start | bytes 3735560 | tf_op jit(solution)/shard_map/ppermute | solution.py:268
  2.7 0.1 collective-permute-start.8
  2.8 0.5 %collective-permute-start = (s32[2,8]{1,0:T(2,128)S(1)}, s32[2,8]{1,0:T(2,128)S(1)}, u32[]{:S(2)}, u32[]{:S(2)}) collective-permute-start(s32[2,8]{1,0:T(2,128)S(1)} %pad_add_fusion.meta), channel_id=1, source_target_pairs={{0,1},{1,0},{2,3},{3,2},{4,5},{5,4},{6,7},{7,6},{8,9},{9,8},{10,11... | collective-permute-start | bytes 200 | tf_op jit(solution)/shard_map/ppermute | solution.py:267
  3.3 3.0 %shard_map.59 = (f32[4,2592,128]{2,1,0:T(8,128)S(1)}, f32[8,4,216,128]{3,2,1,0:T(8,128)S(1)}, f32[8,8,128]{2,1,0:T(8,128)S(1)}) custom-call(s32[2,8]{1,0:T(2,128)S(1)} %pad_add_fusion.meta, f32[12,110592]{1,0:T(8,128)} %table.1, bf16[8,8,216,128]{3,2,1,0:T(8,128)(2,1)} %bitcast.18), custom_call_target="tpu_custom_call" | custom-call | flops 16777216 | bytes 16777216 | tf_op jit(solution)/shard_map/pallas_call | solution.py:221
  6.3 0.0 collective-permute-done.got_meta
  6.3 0.0 collective-permute-done.1.got
  6.3 1.3 %shard_map.61 = (s16[2,4,152,128]{3,2,1,0:T(8,128)(2,1)S(1)}, s16[2,4,152,128]{3,2,1,0:T(8,128)(2,1)S(1)}, s16[2,4,152,128]{3,2,1,0:T(8,128)(2,1)S(1)}, s16[2,4,152,128]{3,2,1,0:T(8,128)(2,1)S(1)}) custom-call(s32[2,8]{1,0:T(2,128)S(1)} %collective-permute-done.got_meta, bf16[8,4,152,128]{3,2,1,0:T(8,128)(2,1)S(1)} %collective-permute-done.1.got, ...), custom_call_target="tpu_custom_call" | custom-call | flops 4194304 | bytes 4194304 | tf_op jit(solution)/shard_map/pallas_call | solution.py:221
  7.7 2.7 %collective-permute-start.2 = (s16[2,4,152,128]{3,2,1,0:T(8,128)(2,1)S(1)}, s16[2,4,152,128]{3,2,1,0:T(8,128)(2,1)S(1)}, u32[]{:S(2)}, u32[]{:S(2)}) collective-permute-start(s16[2,4,152,128]{3,2,1,0:T(8,128)(2,1)S(1)} %get-tuple-element.30), channel_id=1, source_target_pairs={{0,8},{8,0},{16,24},{24,16},{1,9},{9,1},{17,25},{25,17},{2,10},{10... | collective-permute-start | bytes 933896 | tf_op jit(solution)/shard_map/ppermute | solution.py:298
  10.4 1.5 %collective-permute-start.3 = (s16[2,4,152,128]{3,2,1,0:T(8,128)(2,1)S(1)}, s16[2,4,152,128]{3,2,1,0:T(8,128)(2,1)S(1)}, u32[]{:S(2)}, u32[]{:S(2)}) collective-permute-start(s16[2,4,152,128]{3,2,1,0:T(8,128)(2,1)S(1)} %get-tuple-element.31), channel_id=1, source_target_pairs={{0,16},{8,24},{16,0},{24,8},{1,17},{9,25},{17,1},{25,9},{2,18},{10... | collective-permute-start | bytes 933896 | tf_op jit(solution)/shard_map/ppermute | solution.py:298
  11.9 0.0 collective-permute-start.4
  11.9 0.0 collective-permute-done.8.got
  11.9 0.6 %shard_map.63 = (s16[8,72,128]{2,1,0:T(8,128)(2,1)S(1)}, s16[8,72,128]{2,1,0:T(8,128)(2,1)S(1)}, s16[8,72,128]{2,1,0:T(8,128)(2,1)S(1)}, s16[8,72,128]{2,1,0:T(8,128)(2,1)S(1)}) custom-call(s32[2,8]{1,0:T(2,128)S(1)} %collective-permute-done.got_meta, bf16[8,4,72,128]{3,2,1,0:T(8,128)(2,1)S(1)} %collective-permute-done.8.got, ...), custom_call_target="tpu_custom_call" | custom-call | flops 4194304 | bytes 4194304 | tf_op jit(solution)/shard_map/pallas_call | solution.py:221
  12.6 3.1 %collective-permute-start.10 = (s16[8,72,128]{2,1,0:T(8,128)(2,1)S(1)}, s16[8,72,128]{2,1,0:T(8,128)(2,1)S(1)}, u32[]{:S(2)}, u32[]{:S(2)}) collective-permute-start(s16[8,72,128]{2,1,0:T(8,128)(2,1)S(1)} %get-tuple-element.40), channel_id=1, source_target_pairs={{0,4},{1,5},{2,6},{3,7},{4,0},{5,1},{6,2},{7,3},{8,12},{9,13},{10,... | collective-permute-start | bytes 442376 | tf_op jit(solution)/shard_map/ppermute | solution.py:298
  15.7 1.4 %collective-permute-start.11 = (s16[8,72,128]{2,1,0:T(8,128)(2,1)S(1)}, s16[8,72,128]{2,1,0:T(8,128)(2,1)S(1)}, u32[]{:S(2)}, u32[]{:S(2)}) collective-permute-start(s16[8,72,128]{2,1,0:T(8,128)(2,1)S(1)} %get-tuple-element.41), channel_id=1, source_target_pairs={{0,6},{1,7},{2,4},{3,5},{4,2},{5,3},{6,0},{7,1},{8,14},{9,15},{10,... | collective-permute-start | bytes 442376 | tf_op jit(solution)/shard_map/ppermute | solution.py:298
  17.1 1.5 %collective-permute-done.2.refs_1_ = s16[2,4,152,128]{3,2,1,0:T(8,128)(2,1)S(1)} collective-permute-done((s16[2,4,152,128]{3,2,1,0:T(8,128)(2,1)S(1)}, s16[2,4,152,128]{3,2,1,0:T(8,128)(2,1)S(1)}, u32[]{:S(2)}, u32[]{:S(2)}) %collective-permute-start.2) | collective-permute-done | bytes 311328 | tf_op jit(solution)/shard_map/ppermute | solution.py:298
  18.6 2.1 %collective-permute-start.9 = (s16[8,72,128]{2,1,0:T(8,128)(2,1)S(1)}, s16[8,72,128]{2,1,0:T(8,128)(2,1)S(1)}, u32[]{:S(2)}, u32[]{:S(2)}) collective-permute-start(s16[8,72,128]{2,1,0:T(8,128)(2,1)S(1)} %get-tuple-element.39), channel_id=1, source_target_pairs={{0,2},{1,3},{2,0},{3,1},{4,6},{5,7},{6,4},{7,5},{8,10},{9,11},{10,... | collective-permute-start | bytes 442376 | tf_op jit(solution)/shard_map/ppermute | solution.py:298
  20.7 5.7 %collective-permute-done.3.refs_2_ = s16[2,4,152,128]{3,2,1,0:T(8,128)(2,1)S(1)} collective-permute-done((s16[2,4,152,128]{3,2,1,0:T(8,128)(2,1)S(1)}, s16[2,4,152,128]{3,2,1,0:T(8,128)(2,1)S(1)}, u32[]{:S(2)}, u32[]{:S(2)}) %collective-permute-start.3) | collective-permute-done | bytes 311328 | tf_op jit(solution)/shard_map/ppermute | solution.py:298
  26.4 0.0 collective-permute-done.4.refs_3_
  26.4 0.4 %shard_map.62 = (s16[2,152,128]{2,1,0:T(8,128)(2,1)S(1)}, s16[2,152,128]{2,1,0:T(8,128)(2,1)S(1)}, s16[2,152,128]{2,1,0:T(8,128)(2,1)S(1)}, s16[2,152,128]{2,1,0:T(8,128)(2,1)S(1)}) custom-call(s16[2,4,152,128]{3,2,1,0:T(8,128)(2,1)S(1)} %get-tuple-element.29.refs_0_, s16[2,4,152,128]{3,2,1,0:T(8,128)(2,1)S(1)} %collective-permute-done.2.refs_1_, ...), custom_call_target="tpu_custom_call" | custom-call | flops 4194304 | bytes 4194304 | tf_op jit(solution)/shard_map/pallas_call | solution.py:221
  26.8 1.6 %collective-permute-start.5 = (s16[2,152,128]{2,1,0:T(8,128)(2,1)S(1)}, s16[2,152,128]{2,1,0:T(8,128)(2,1)S(1)}, u32[]{:S(2)}, u32[]{:S(2)}) collective-permute-start(s16[2,152,128]{2,1,0:T(8,128)(2,1)S(1)} %get-tuple-element.34), channel_id=1, source_target_pairs={{0,2},{1,3},{2,0},{3,1},{4,6},{5,7},{6,4},{7,5},{8,10},{9,11},{10,... | collective-permute-start | bytes 233480 | tf_op jit(solution)/shard_map/ppermute | solution.py:298
  28.5 2.6 %collective-permute-start.6 = (s16[2,152,128]{2,1,0:T(8,128)(2,1)S(1)}, s16[2,152,128]{2,1,0:T(8,128)(2,1)S(1)}, u32[]{:S(2)}, u32[]{:S(2)}) collective-permute-start(s16[2,152,128]{2,1,0:T(8,128)(2,1)S(1)} %get-tuple-element.35), channel_id=1, source_target_pairs={{0,4},{1,5},{2,6},{3,7},{4,0},{5,1},{6,2},{7,3},{8,12},{9,13},{10,... | collective-permute-start | bytes 233480 | tf_op jit(solution)/shard_map/ppermute | solution.py:298
  31.1 0.2 collective-permute-start.7
  31.3 0.3 shard_map.64
  31.6 1.3 %collective-permute-start.12 = (s16[2,72,128]{2,1,0:T(8,128)(2,1)S(1)}, s16[2,72,128]{2,1,0:T(8,128)(2,1)S(1)}, u32[]{:S(2)}, u32[]{:S(2)}) collective-permute-start(s16[2,72,128]{2,1,0:T(8,128)(2,1)S(1)} %get-tuple-element.43), channel_id=1, source_target_pairs={{0,8},{8,0},{16,24},{24,16},{1,9},{9,1},{17,25},{25,17},{2,10},{10... | collective-permute-start | bytes 110600 | tf_op jit(solution)/shard_map/ppermute | solution.py:298
  32.8 0.8 %collective-permute-start.13 = (s16[2,72,128]{2,1,0:T(8,128)(2,1)S(1)}, s16[2,72,128]{2,1,0:T(8,128)(2,1)S(1)}, u32[]{:S(2)}, u32[]{:S(2)}) collective-permute-start(s16[2,72,128]{2,1,0:T(8,128)(2,1)S(1)} %get-tuple-element.44), channel_id=1, source_target_pairs={{0,16},{8,24},{16,0},{24,8},{1,17},{9,25},{17,1},{25,9},{2,18},{10... | collective-permute-start | bytes 110600 | tf_op jit(solution)/shard_map/ppermute | solution.py:298
  33.7 1.9 %collective-permute-done.12.refs_5_ = s16[2,72,128]{2,1,0:T(8,128)(2,1)S(1)} collective-permute-done((s16[2,72,128]{2,1,0:T(8,128)(2,1)S(1)}, s16[2,72,128]{2,1,0:T(8,128)(2,1)S(1)}, u32[]{:S(2)}, u32[]{:S(2)}) %collective-permute-start.12) | collective-permute-done | bytes 36896 | tf_op jit(solution)/shard_map/ppermute | solution.py:298
  35.6 1.5 %collective-permute-start.14 = (s16[2,72,128]{2,1,0:T(8,128)(2,1)S(1)}, s16[2,72,128]{2,1,0:T(8,128)(2,1)S(1)}, u32[]{:S(2)}, u32[]{:S(2)}) collective-permute-start(s16[2,72,128]{2,1,0:T(8,128)(2,1)S(1)} %get-tuple-element.45), channel_id=1, source_target_pairs={{0,24},{8,16},{16,8},{24,0},{1,25},{9,17},{17,9},{25,1},{2,26},{10... | collective-permute-start | bytes 110600 | tf_op jit(solution)/shard_map/ppermute | solution.py:298
  37.1 3.4 %collective-permute-done.14.refs_7_ = s16[2,72,128]{2,1,0:T(8,128)(2,1)S(1)} collective-permute-done((s16[2,72,128]{2,1,0:T(8,128)(2,1)S(1)}, s16[2,72,128]{2,1,0:T(8,128)(2,1)S(1)}, u32[]{:S(2)}, u32[]{:S(2)}) %collective-permute-start.14) | collective-permute-done | bytes 36896 | tf_op jit(solution)/shard_map/ppermute | solution.py:298
  40.4 0.0 collective-permute-done.6.refs_2_
  40.4 0.0 collective-permute-done.7.refs_3_
  40.5 1.1 %shard_map.65 = (f32[2,216,128]{2,1,0:T(8,128)}, f32[216,128]{1,0:T(8,128)}) custom-call(f32[4,2592,128]{2,1,0:T(8,128)S(1)} %get-tuple-element.25.weights, s16[2,152,128]{2,1,0:T(8,128)(2,1)S(1)} %get-tuple-element.33.refs_0_, s16[2,152,128]{2,1,0:T(8,128)(2,1)S(1)} %collective-permute-done.5.refs_1_, ...), custom_call_target="tpu_custom_call" | custom-call | flops 4194304 | bytes 4194304 | tf_op jit(solution)/shard_map/pallas_call | solution.py:221
  (10 shorter events, 0.0 us)
Async XLA Ops:
  0.6 2.2 %copy-start.1 = (s32[8,1]{0,1:T(1,128)S(1)}, s32[8,1]{0,1:T(1,128)}, u32[]{:S(2)}) copy-start(s32[8,1]{0,1:T(1,128)} %param.5) | copy-start | bytes 100
  0.6 2.2 %copy-start = (s32[8]{0:T(128)S(1)}, s32[8]{0:T(128)}, u32[]{:S(2)}) copy-start(s32[8]{0:T(128)} %param.6) | copy-start | bytes 100
  2.2 4.2 %collective-permute-start.1 = (bf16[8,4,152,128]{3,2,1,0:T(8,128)(2,1)S(1)}, bf16[8,4,152,128]{3,2,1,0:T(8,128)(2,1)S(1)}, u32[]{:S(2)}, u32[]{:S(2)}) collective-permute-start(bf16[8,4,152,128]{3,2,1,0:T(8,128)(2,1)S(1)} %get-tuple-element.26), channel_id=1, source_target_pairs={{0,1},{1,0},{2,3},{3,2},{4,5},{5,4},{6,7},{7,6},{8,9},{9,8},{10,11... | collective-permute-start | bytes 3735560 | tf_op jit(solution)/shard_map/ppermute | solution.py:268
  2.7 9.2 %collective-permute-start.8 = (bf16[8,4,72,128]{3,2,1,0:T(8,128)(2,1)S(1)}, bf16[8,4,72,128]{3,2,1,0:T(8,128)(2,1)S(1)}, u32[]{:S(2)}, u32[]{:S(2)}) collective-permute-start(bf16[8,4,72,128]{3,2,1,0:T(8,128)(2,1)S(1)} %get-tuple-element.37), channel_id=1, source_target_pairs={{0,1},{1,0},{2,3},{3,2},{4,5},{5,4},{6,7},{7,6},{8,9},{9,8},{10,11... | collective-permute-start | bytes 1769480 | tf_op jit(solution)/shard_map/ppermute | solution.py:268
  2.8 3.5 %collective-permute-start = (s32[2,8]{1,0:T(2,128)S(1)}, s32[2,8]{1,0:T(2,128)S(1)}, u32[]{:S(2)}, u32[]{:S(2)}) collective-permute-start(s32[2,8]{1,0:T(2,128)S(1)} %pad_add_fusion.meta), channel_id=1, source_target_pairs={{0,1},{1,0},{2,3},{3,2},{4,5},{5,4},{6,7},{7,6},{8,9},{9,8},{10,11... | collective-permute-start | bytes 200 | tf_op jit(solution)/shard_map/ppermute | solution.py:267
  7.7 10.9 %collective-permute-start.2 = (s16[2,4,152,128]{3,2,1,0:T(8,128)(2,1)S(1)}, s16[2,4,152,128]{3,2,1,0:T(8,128)(2,1)S(1)}, u32[]{:S(2)}, u32[]{:S(2)}) collective-permute-start(s16[2,4,152,128]{3,2,1,0:T(8,128)(2,1)S(1)} %get-tuple-element.30), channel_id=1, source_target_pairs={{0,8},{8,0},{16,24},{24,16},{1,9},{9,1},{17,25},{25,17},{2,10},{10... | collective-permute-start | bytes 933896 | tf_op jit(solution)/shard_map/ppermute | solution.py:298
  10.4 16.0 %collective-permute-start.3 = (s16[2,4,152,128]{3,2,1,0:T(8,128)(2,1)S(1)}, s16[2,4,152,128]{3,2,1,0:T(8,128)(2,1)S(1)}, u32[]{:S(2)}, u32[]{:S(2)}) collective-permute-start(s16[2,4,152,128]{3,2,1,0:T(8,128)(2,1)S(1)} %get-tuple-element.31), channel_id=1, source_target_pairs={{0,16},{8,24},{16,0},{24,8},{1,17},{9,25},{17,1},{25,9},{2,18},{10... | collective-permute-start | bytes 933896 | tf_op jit(solution)/shard_map/ppermute | solution.py:298
  11.9 14.5 %collective-permute-start.4 = (s16[2,4,152,128]{3,2,1,0:T(8,128)(2,1)S(1)}, s16[2,4,152,128]{3,2,1,0:T(8,128)(2,1)S(1)}, u32[]{:S(2)}, u32[]{:S(2)}) collective-permute-start(s16[2,4,152,128]{3,2,1,0:T(8,128)(2,1)S(1)} %get-tuple-element.32), channel_id=1, source_target_pairs={{0,24},{8,16},{16,8},{24,0},{1,25},{9,17},{17,9},{25,1},{2,26},{10... | collective-permute-start | bytes 933896 | tf_op jit(solution)/shard_map/ppermute | solution.py:298
  12.6 18.5 %collective-permute-start.10 = (s16[8,72,128]{2,1,0:T(8,128)(2,1)S(1)}, s16[8,72,128]{2,1,0:T(8,128)(2,1)S(1)}, u32[]{:S(2)}, u32[]{:S(2)}) collective-permute-start(s16[8,72,128]{2,1,0:T(8,128)(2,1)S(1)} %get-tuple-element.40), channel_id=1, source_target_pairs={{0,4},{1,5},{2,6},{3,7},{4,0},{5,1},{6,2},{7,3},{8,12},{9,13},{10,... | collective-permute-start | bytes 442376 | tf_op jit(solution)/shard_map/ppermute | solution.py:298
  15.7 15.6 %collective-permute-start.11 = (s16[8,72,128]{2,1,0:T(8,128)(2,1)S(1)}, s16[8,72,128]{2,1,0:T(8,128)(2,1)S(1)}, u32[]{:S(2)}, u32[]{:S(2)}) collective-permute-start(s16[8,72,128]{2,1,0:T(8,128)(2,1)S(1)} %get-tuple-element.41), channel_id=1, source_target_pairs={{0,6},{1,7},{2,4},{3,5},{4,2},{5,3},{6,0},{7,1},{8,14},{9,15},{10,... | collective-permute-start | bytes 442376 | tf_op jit(solution)/shard_map/ppermute | solution.py:298
  18.6 12.7 %collective-permute-start.9 = (s16[8,72,128]{2,1,0:T(8,128)(2,1)S(1)}, s16[8,72,128]{2,1,0:T(8,128)(2,1)S(1)}, u32[]{:S(2)}, u32[]{:S(2)}) collective-permute-start(s16[8,72,128]{2,1,0:T(8,128)(2,1)S(1)} %get-tuple-element.39), channel_id=1, source_target_pairs={{0,2},{1,3},{2,0},{3,1},{4,6},{5,7},{6,4},{7,5},{8,10},{9,11},{10,... | collective-permute-start | bytes 442376 | tf_op jit(solution)/shard_map/ppermute | solution.py:298
  26.8 13.6 %collective-permute-start.5 = (s16[2,152,128]{2,1,0:T(8,128)(2,1)S(1)}, s16[2,152,128]{2,1,0:T(8,128)(2,1)S(1)}, u32[]{:S(2)}, u32[]{:S(2)}) collective-permute-start(s16[2,152,128]{2,1,0:T(8,128)(2,1)S(1)} %get-tuple-element.34), channel_id=1, source_target_pairs={{0,2},{1,3},{2,0},{3,1},{4,6},{5,7},{6,4},{7,5},{8,10},{9,11},{10,... | collective-permute-start | bytes 233480 | tf_op jit(solution)/shard_map/ppermute | solution.py:298
  28.5 12.0 %collective-permute-start.6 = (s16[2,152,128]{2,1,0:T(8,128)(2,1)S(1)}, s16[2,152,128]{2,1,0:T(8,128)(2,1)S(1)}, u32[]{:S(2)}, u32[]{:S(2)}) collective-permute-start(s16[2,152,128]{2,1,0:T(8,128)(2,1)S(1)} %get-tuple-element.35), channel_id=1, source_target_pairs={{0,4},{1,5},{2,6},{3,7},{4,0},{5,1},{6,2},{7,3},{8,12},{9,13},{10,... | collective-permute-start | bytes 233480 | tf_op jit(solution)/shard_map/ppermute | solution.py:298
  31.1 9.4 %collective-permute-start.7 = (s16[2,152,128]{2,1,0:T(8,128)(2,1)S(1)}, s16[2,152,128]{2,1,0:T(8,128)(2,1)S(1)}, u32[]{:S(2)}, u32[]{:S(2)}) collective-permute-start(s16[2,152,128]{2,1,0:T(8,128)(2,1)S(1)} %get-tuple-element.36), channel_id=1, source_target_pairs={{0,6},{1,7},{2,4},{3,5},{4,2},{5,3},{6,0},{7,1},{8,14},{9,15},{10,... | collective-permute-start | bytes 233480 | tf_op jit(solution)/shard_map/ppermute | solution.py:298
  31.6 4.0 %collective-permute-start.12 = (s16[2,72,128]{2,1,0:T(8,128)(2,1)S(1)}, s16[2,72,128]{2,1,0:T(8,128)(2,1)S(1)}, u32[]{:S(2)}, u32[]{:S(2)}) collective-permute-start(s16[2,72,128]{2,1,0:T(8,128)(2,1)S(1)} %get-tuple-element.43), channel_id=1, source_target_pairs={{0,8},{8,0},{16,24},{24,16},{1,9},{9,1},{17,25},{25,17},{2,10},{10... | collective-permute-start | bytes 110600 | tf_op jit(solution)/shard_map/ppermute | solution.py:298
  32.8 4.2 %collective-permute-start.13 = (s16[2,72,128]{2,1,0:T(8,128)(2,1)S(1)}, s16[2,72,128]{2,1,0:T(8,128)(2,1)S(1)}, u32[]{:S(2)}, u32[]{:S(2)}) collective-permute-start(s16[2,72,128]{2,1,0:T(8,128)(2,1)S(1)} %get-tuple-element.44), channel_id=1, source_target_pairs={{0,16},{8,24},{16,0},{24,8},{1,17},{9,25},{17,1},{25,9},{2,18},{10... | collective-permute-start | bytes 110600 | tf_op jit(solution)/shard_map/ppermute | solution.py:298
  35.6 4.9 %collective-permute-start.14 = (s16[2,72,128]{2,1,0:T(8,128)(2,1)S(1)}, s16[2,72,128]{2,1,0:T(8,128)(2,1)S(1)}, u32[]{:S(2)}, u32[]{:S(2)}) collective-permute-start(s16[2,72,128]{2,1,0:T(8,128)(2,1)S(1)} %get-tuple-element.45), channel_id=1, source_target_pairs={{0,24},{8,16},{16,8},{24,0},{1,25},{9,17},{17,9},{25,1},{2,26},{10... | collective-permute-start | bytes 110600 | tf_op jit(solution)/shard_map/ppermute | solution.py:298

commit v2 on v1

--- a/solution.py
+++ b/solution.py
@@ -15,7 +15,7 @@
 CORES = 2
 PARTS = 2
 STEPS = 8
-CUT = 67
+CUT = 63
 TOP = 32000.0
 LEAST = 1e-30
 VMEM = pl.BlockSpec(memory_space=pltpu.VMEM)
@@ -308,7 +308,8 @@
 
     size = [high - low for low, high in cuts]
     head = over("cls", cls_moves, chip(0, False, [array((CLS_GROUP, n_z, size[0]), jnp.int16)] * n_cls))
-    ends = over("dom", z_moves, chip(1, True, [array((n_class, size[1]), jnp.int16)] * n_z))
+    ends = chip(1, True, [array((n_class, size[1]), jnp.int16)] * n_z)
+    ends = over("dom", z_moves, ends)
     head = fold(sum_cls, n_cls, head, [array((CLS_GROUP, size[0]), jnp.int16)] * n_z)
     head = over("dom", z_moves, head)
     ends = fold(sum_z, n_z, ends, [array((CLS_GROUP, size[1]), jnp.int16)] * n_cls)

time: 41.7 us -> 43 us (1.031)
  waiting for transfers between devices: 12.5 us -> 15.3 us
  starting transfers between devices: 20.1 us -> 18.5 us
    ppermute x12, waiting for transfers between devices: 12.5 us -> 15.3 us  [over(): moved[i] = lax.ppermute(arrays[i], axis, moves[i])]
    ppermute x12, starting transfers between devices: 18.9 us -> 17.4 us  [over(): moved[i] = lax.ppermute(arrays[i], axis, moves[i])]
  transfers between devices with their start and end apart: 15 -> 15, of which waited for: 4 -> 4; matrix products, arithmetic and copies ran while one was open for 0% -> 0% of each run, Pallas kernels for 14% -> 13%
where the time goes in v2:
time: 43 us; the launch traced here: 42.9 us
  starting transfers between devices  18.5 us (43%)
  waiting for transfers between devices  15.3 us (36%)
  Pallas kernels  8.3 us (19%)
  between operations  0.72 us (2%)
    ppermute x12, starting transfers between devices, over(): moved[i] = lax.ppermute(arrays[i], axis, moves[i])  17.4 us
    ppermute x12, waiting for transfers between devices, over(): moved[i] = lax.ppermute(arrays[i], axis, moves[i])  15.3 us
    pallas_call x7, Pallas kernels, call(): pl.pallas_call(body, out_shape=shapes, in_specs=specs, out_specs=[VMEM] *...  8.3 us
  transfers between devices with their start and end apart: 15, of which 4 were waited for; matrix products, arithmetic and copies ran while one was open for 0% of the time, Pallas kernels for 13%

profile of v2, /device:TPU:0, one launch (start us, length us, event | category | flops | bytes accessed | tf_op | source)
XLA Modules:
  0.0 42.9 jit_solution(15795523985647684343)
XLA Ops:
  0.6 1.5 %shard_map.60 = (bf16[8,4,144,128]{3,2,1,0:T(8,128)(2,1)S(1)}, bf16[8,4,80,128]{3,2,1,0:T(8,128)(2,1)S(1)}) custom-call(bf16[8,8,216,128]{3,2,1,0:T(8,128)(2,1)} %bitcast.17), custom_call_target="tpu_custom_call" | custom-call | flops 4194304 | bytes 4194304 | tf_op jit(solution)/shard_map/pallas_call | solution.py:221
  2.2 0.6 %collective-permute-start.1 = (bf16[8,4,144,128]{3,2,1,0:T(8,128)(2,1)S(1)}, bf16[8,4,144,128]{3,2,1,0:T(8,128)(2,1)S(1)}, u32[]{:S(2)}, u32[]{:S(2)}) collective-permute-start(bf16[8,4,144,128]{3,2,1,0:T(8,128)(2,1)S(1)} %get-tuple-element.26), channel_id=1, source_target_pairs={{0,1},{1,0},{2,3},{3,2},{4,5},{5,4},{6,7},{7,6},{8,9},{9,8},{10,11... | collective-permute-start | bytes 3538952 | tf_op jit(solution)/shard_map/ppermute | solution.py:268
  2.7 0.1 collective-permute-start.8
  2.8 0.5 %collective-permute-start = (s32[2,8]{1,0:T(2,128)S(1)}, s32[2,8]{1,0:T(2,128)S(1)}, u32[]{:S(2)}, u32[]{:S(2)}) collective-permute-start(s32[2,8]{1,0:T(2,128)S(1)} %pad_add_fusion.meta), channel_id=1, source_target_pairs={{0,1},{1,0},{2,3},{3,2},{4,5},{5,4},{6,7},{7,6},{8,9},{9,8},{10,11... | collective-permute-start | bytes 200 | tf_op jit(solution)/shard_map/ppermute | solution.py:267
  3.3 3.0 %shard_map.59 = (f32[4,2592,128]{2,1,0:T(8,128)S(1)}, f32[8,4,216,128]{3,2,1,0:T(8,128)S(1)}, f32[8,8,128]{2,1,0:T(8,128)S(1)}) custom-call(s32[2,8]{1,0:T(2,128)S(1)} %pad_add_fusion.meta, f32[12,110592]{1,0:T(8,128)} %table.1, bf16[8,8,216,128]{3,2,1,0:T(8,128)(2,1)} %bitcast.18), custom_call_target="tpu_custom_call" | custom-call | flops 16777216 | bytes 16777216 | tf_op jit(solution)/shard_map/pallas_call | solution.py:221
  6.3 0.0 collective-permute-done.got_meta
  6.3 0.0 collective-permute-done.8.got
  6.3 0.7 %shard_map.63 = (s16[8,80,128]{2,1,0:T(8,128)(2,1)S(1)}, s16[8,80,128]{2,1,0:T(8,128)(2,1)S(1)}, s16[8,80,128]{2,1,0:T(8,128)(2,1)S(1)}, s16[8,80,128]{2,1,0:T(8,128)(2,1)S(1)}) custom-call(s32[2,8]{1,0:T(2,128)S(1)} %collective-permute-done.got_meta, bf16[8,4,80,128]{3,2,1,0:T(8,128)(2,1)S(1)} %collective-permute-done.8.got, ...), custom_call_target="tpu_custom_call" | custom-call | flops 4194304 | bytes 4194304 | tf_op jit(solution)/shard_map/pallas_call | solution.py:221
  7.1 3.8 %collective-permute-start.10 = (s16[8,80,128]{2,1,0:T(8,128)(2,1)S(1)}, s16[8,80,128]{2,1,0:T(8,128)(2,1)S(1)}, u32[]{:S(2)}, u32[]{:S(2)}) collective-permute-start(s16[8,80,128]{2,1,0:T(8,128)(2,1)S(1)} %get-tuple-element.40), channel_id=1, source_target_pairs={{0,4},{1,5},{2,6},{3,7},{4,0},{5,1},{6,2},{7,3},{8,12},{9,13},{10,... | collective-permute-start | bytes 491528 | tf_op jit(solution)/shard_map/ppermute | solution.py:298
  10.9 1.2 %shard_map.61 = (s16[2,4,144,128]{3,2,1,0:T(8,128)(2,1)S(1)}, s16[2,4,144,128]{3,2,1,0:T(8,128)(2,1)S(1)}, s16[2,4,144,128]{3,2,1,0:T(8,128)(2,1)S(1)}, s16[2,4,144,128]{3,2,1,0:T(8,128)(2,1)S(1)}) custom-call(s32[2,8]{1,0:T(2,128)S(1)} %collective-permute-done.got_meta, bf16[8,4,144,128]{3,2,1,0:T(8,128)(2,1)S(1)} %collective-permute-done.1.got, ...), custom_call_target="tpu_custom_call" | custom-call | flops 4194304 | bytes 4194304 | tf_op jit(solution)/shard_map/pallas_call | solution.py:221
  12.1 1.6 %collective-permute-start.2 = (s16[2,4,144,128]{3,2,1,0:T(8,128)(2,1)S(1)}, s16[2,4,144,128]{3,2,1,0:T(8,128)(2,1)S(1)}, u32[]{:S(2)}, u32[]{:S(2)}) collective-permute-start(s16[2,4,144,128]{3,2,1,0:T(8,128)(2,1)S(1)} %get-tuple-element.30), channel_id=1, source_target_pairs={{0,8},{8,0},{16,24},{24,16},{1,9},{9,1},{17,25},{25,17},{2,10},{10... | collective-permute-start | bytes 884744 | tf_op jit(solution)/shard_map/ppermute | solution.py:298
  13.7 1.5 %collective-permute-start.3 = (s16[2,4,144,128]{3,2,1,0:T(8,128)(2,1)S(1)}, s16[2,4,144,128]{3,2,1,0:T(8,128)(2,1)S(1)}, u32[]{:S(2)}, u32[]{:S(2)}) collective-permute-start(s16[2,4,144,128]{3,2,1,0:T(8,128)(2,1)S(1)} %get-tuple-element.31), channel_id=1, source_target_pairs={{0,16},{8,24},{16,0},{24,8},{1,17},{9,25},{17,1},{25,9},{2,18},{10... | collective-permute-start | bytes 884744 | tf_op jit(solution)/shard_map/ppermute | solution.py:298
  15.2 0.5 %collective-permute-start.4 = (s16[2,4,144,128]{3,2,1,0:T(8,128)(2,1)S(1)}, s16[2,4,144,128]{3,2,1,0:T(8,128)(2,1)S(1)}, u32[]{:S(2)}, u32[]{:S(2)}) collective-permute-start(s16[2,4,144,128]{3,2,1,0:T(8,128)(2,1)S(1)} %get-tuple-element.32), channel_id=1, source_target_pairs={{0,24},{8,16},{16,8},{24,0},{1,25},{9,17},{17,9},{25,1},{2,26},{10... | collective-permute-start | bytes 884744 | tf_op jit(solution)/shard_map/ppermute | solution.py:298
  15.7 1.4 %collective-permute-start.11 = (s16[8,80,128]{2,1,0:T(8,128)(2,1)S(1)}, s16[8,80,128]{2,1,0:T(8,128)(2,1)S(1)}, u32[]{:S(2)}, u32[]{:S(2)}) collective-permute-start(s16[8,80,128]{2,1,0:T(8,128)(2,1)S(1)} %get-tuple-element.41), channel_id=1, source_target_pairs={{0,6},{1,7},{2,4},{3,5},{4,2},{5,3},{6,0},{7,1},{8,14},{9,15},{10,... | collective-permute-start | bytes 491528 | tf_op jit(solution)/shard_map/ppermute | solution.py:298
  17.1 5.9 %collective-permute-done.10.refs_2_ = s16[8,80,128]{2,1,0:T(8,128)(2,1)S(1)} collective-permute-done((s16[8,80,128]{2,1,0:T(8,128)(2,1)S(1)}, s16[8,80,128]{2,1,0:T(8,128)(2,1)S(1)}, u32[]{:S(2)}, u32[]{:S(2)}) %collective-permute-start.10) | collective-permute-done | bytes 163872 | tf_op jit(solution)/shard_map/ppermute | solution.py:298
  23.0 0.4 %collective-permute-start.9 = (s16[8,80,128]{2,1,0:T(8,128)(2,1)S(1)}, s16[8,80,128]{2,1,0:T(8,128)(2,1)S(1)}, u32[]{:S(2)}, u32[]{:S(2)}) collective-permute-start(s16[8,80,128]{2,1,0:T(8,128)(2,1)S(1)} %get-tuple-element.39), channel_id=1, source_target_pairs={{0,2},{1,3},{2,0},{3,1},{4,6},{5,7},{6,4},{7,5},{8,10},{9,11},{10,... | collective-permute-start | bytes 491528 | tf_op jit(solution)/shard_map/ppermute | solution.py:298
  23.4 0.0 collective-permute-done.11.refs_3_
  23.4 4.9 %collective-permute-done.9.refs_1_ = s16[8,80,128]{2,1,0:T(8,128)(2,1)S(1)} collective-permute-done((s16[8,80,128]{2,1,0:T(8,128)(2,1)S(1)}, s16[8,80,128]{2,1,0:T(8,128)(2,1)S(1)}, u32[]{:S(2)}, u32[]{:S(2)}) %collective-permute-start.9) | collective-permute-done | bytes 163872 | tf_op jit(solution)/shard_map/ppermute | solution.py:298
  28.3 0.3 shard_map.64
  28.5 1.9 %collective-permute-start.12 = (s16[2,80,128]{2,1,0:T(8,128)(2,1)S(1)}, s16[2,80,128]{2,1,0:T(8,128)(2,1)S(1)}, u32[]{:S(2)}, u32[]{:S(2)}) collective-permute-start(s16[2,80,128]{2,1,0:T(8,128)(2,1)S(1)} %get-tuple-element.43), channel_id=1, source_target_pairs={{0,8},{8,0},{16,24},{24,16},{1,9},{9,1},{17,25},{25,17},{2,10},{10... | collective-permute-start | bytes 122888 | tf_op jit(solution)/shard_map/ppermute | solution.py:298
  30.4 0.0 collective-permute-done.2.refs_1_
  30.4 0.0 collective-permute-done.3.refs_2_
  30.4 0.0 collective-permute-done.4.refs_3_
  30.4 0.4 %shard_map.62 = (s16[2,144,128]{2,1,0:T(8,128)(2,1)S(1)}, s16[2,144,128]{2,1,0:T(8,128)(2,1)S(1)}, s16[2,144,128]{2,1,0:T(8,128)(2,1)S(1)}, s16[2,144,128]{2,1,0:T(8,128)(2,1)S(1)}) custom-call(s16[2,4,144,128]{3,2,1,0:T(8,128)(2,1)S(1)} %get-tuple-element.29.refs_0_, s16[2,4,144,128]{3,2,1,0:T(8,128)(2,1)S(1)} %collective-permute-done.2.refs_1_, ...), custom_call_target="tpu_custom_call" | custom-call | flops 4194304 | bytes 4194304 | tf_op jit(solution)/shard_map/pallas_call | solution.py:221
  30.9 1.0 %collective-permute-start.5 = (s16[2,144,128]{2,1,0:T(8,128)(2,1)S(1)}, s16[2,144,128]{2,1,0:T(8,128)(2,1)S(1)}, u32[]{:S(2)}, u32[]{:S(2)}) collective-permute-start(s16[2,144,128]{2,1,0:T(8,128)(2,1)S(1)} %get-tuple-element.34), channel_id=1, source_target_pairs={{0,2},{1,3},{2,0},{3,1},{4,6},{5,7},{6,4},{7,5},{8,10},{9,11},{10,... | collective-permute-start | bytes 221192 | tf_op jit(solution)/shard_map/ppermute | solution.py:298
  31.8 3.4 %collective-permute-start.6 = (s16[2,144,128]{2,1,0:T(8,128)(2,1)S(1)}, s16[2,144,128]{2,1,0:T(8,128)(2,1)S(1)}, u32[]{:S(2)}, u32[]{:S(2)}) collective-permute-start(s16[2,144,128]{2,1,0:T(8,128)(2,1)S(1)} %get-tuple-element.35), channel_id=1, source_target_pairs={{0,4},{1,5},{2,6},{3,7},{4,0},{5,1},{6,2},{7,3},{8,12},{9,13},{10,... | collective-permute-start | bytes 221192 | tf_op jit(solution)/shard_map/ppermute | solution.py:298
  35.2 0.1 collective-permute-start.7
  35.3 1.5 %collective-permute-start.13 = (s16[2,80,128]{2,1,0:T(8,128)(2,1)S(1)}, s16[2,80,128]{2,1,0:T(8,128)(2,1)S(1)}, u32[]{:S(2)}, u32[]{:S(2)}) collective-permute-start(s16[2,80,128]{2,1,0:T(8,128)(2,1)S(1)} %get-tuple-element.44), channel_id=1, source_target_pairs={{0,16},{8,24},{16,0},{24,8},{1,17},{9,25},{17,1},{25,9},{2,18},{10... | collective-permute-start | bytes 122888 | tf_op jit(solution)/shard_map/ppermute | solution.py:298
  36.8 0.4 collective-permute-start.14
  37.2 2.1 %collective-permute-done.13.refs_6_ = s16[2,80,128]{2,1,0:T(8,128)(2,1)S(1)} collective-permute-done((s16[2,80,128]{2,1,0:T(8,128)(2,1)S(1)}, s16[2,80,128]{2,1,0:T(8,128)(2,1)S(1)}, u32[]{:S(2)}, u32[]{:S(2)}) %collective-permute-start.13) | collective-permute-done | bytes 40992 | tf_op jit(solution)/shard_map/ppermute | solution.py:298
  39.3 2.4 %collective-permute-done.14.refs_7_ = s16[2,80,128]{2,1,0:T(8,128)(2,1)S(1)} collective-permute-done((s16[2,80,128]{2,1,0:T(8,128)(2,1)S(1)}, s16[2,80,128]{2,1,0:T(8,128)(2,1)S(1)}, u32[]{:S(2)}, u32[]{:S(2)}) %collective-permute-start.14) | collective-permute-done | bytes 40992 | tf_op jit(solution)/shard_map/ppermute | solution.py:298
  41.7 1.1 %shard_map.65 = (f32[2,216,128]{2,1,0:T(8,128)}, f32[216,128]{1,0:T(8,128)}) custom-call(f32[4,2592,128]{2,1,0:T(8,128)S(1)} %get-tuple-element.25.weights, s16[2,144,128]{2,1,0:T(8,128)(2,1)S(1)} %get-tuple-element.33.refs_0_, s16[2,144,128]{2,1,0:T(8,128)(2,1)S(1)} %collective-permute-done.5.refs_1_, ...), custom_call_target="tpu_custom_call" | custom-call | flops 4194304 | bytes 4194304 | tf_op jit(solution)/shard_map/pallas_call | solution.py:221
  (10 shorter events, 0.0 us)
Async XLA Ops:
  0.6 2.2 %copy-start.1 = (s32[8,1]{0,1:T(1,128)S(1)}, s32[8,1]{0,1:T(1,128)}, u32[]{:S(2)}) copy-start(s32[8,1]{0,1:T(1,128)} %param.5) | copy-start | bytes 100
  0.6 2.2 %copy-start = (s32[8]{0:T(128)S(1)}, s32[8]{0:T(128)}, u32[]{:S(2)}) copy-start(s32[8]{0:T(128)} %param.6) | copy-start | bytes 100
  2.2 8.7 %collective-permute-start.1 = (bf16[8,4,144,128]{3,2,1,0:T(8,128)(2,1)S(1)}, bf16[8,4,144,128]{3,2,1,0:T(8,128)(2,1)S(1)}, u32[]{:S(2)}, u32[]{:S(2)}) collective-permute-start(bf16[8,4,144,128]{3,2,1,0:T(8,128)(2,1)S(1)} %get-tuple-element.26), channel_id=1, source_target_pairs={{0,1},{1,0},{2,3},{3,2},{4,5},{5,4},{6,7},{7,6},{8,9},{9,8},{10,11... | collective-permute-start | bytes 3538952 | tf_op jit(solution)/shard_map/ppermute | solution.py:268
  2.7 3.6 %collective-permute-start.8 = (bf16[8,4,80,128]{3,2,1,0:T(8,128)(2,1)S(1)}, bf16[8,4,80,128]{3,2,1,0:T(8,128)(2,1)S(1)}, u32[]{:S(2)}, u32[]{:S(2)}) collective-permute-start(bf16[8,4,80,128]{3,2,1,0:T(8,128)(2,1)S(1)} %get-tuple-element.37), channel_id=1, source_target_pairs={{0,1},{1,0},{2,3},{3,2},{4,5},{5,4},{6,7},{7,6},{8,9},{9,8},{10,11... | collective-permute-start | bytes 1966088 | tf_op jit(solution)/shard_map/ppermute | solution.py:268
  2.8 3.5 %collective-permute-start = (s32[2,8]{1,0:T(2,128)S(1)}, s32[2,8]{1,0:T(2,128)S(1)}, u32[]{:S(2)}, u32[]{:S(2)}) collective-permute-start(s32[2,8]{1,0:T(2,128)S(1)} %pad_add_fusion.meta), channel_id=1, source_target_pairs={{0,1},{1,0},{2,3},{3,2},{4,5},{5,4},{6,7},{7,6},{8,9},{9,8},{10,11... | collective-permute-start | bytes 200 | tf_op jit(solution)/shard_map/ppermute | solution.py:267
  7.1 15.9 %collective-permute-start.10 = (s16[8,80,128]{2,1,0:T(8,128)(2,1)S(1)}, s16[8,80,128]{2,1,0:T(8,128)(2,1)S(1)}, u32[]{:S(2)}, u32[]{:S(2)}) collective-permute-start(s16[8,80,128]{2,1,0:T(8,128)(2,1)S(1)} %get-tuple-element.40), channel_id=1, source_target_pairs={{0,4},{1,5},{2,6},{3,7},{4,0},{5,1},{6,2},{7,3},{8,12},{9,13},{10,... | collective-permute-start | bytes 491528 | tf_op jit(solution)/shard_map/ppermute | solution.py:298
  12.1 18.3 %collective-permute-start.2 = (s16[2,4,144,128]{3,2,1,0:T(8,128)(2,1)S(1)}, s16[2,4,144,128]{3,2,1,0:T(8,128)(2,1)S(1)}, u32[]{:S(2)}, u32[]{:S(2)}) collective-permute-start(s16[2,4,144,128]{3,2,1,0:T(8,128)(2,1)S(1)} %get-tuple-element.30), channel_id=1, source_target_pairs={{0,8},{8,0},{16,24},{24,16},{1,9},{9,1},{17,25},{25,17},{2,10},{10... | collective-permute-start | bytes 884744 | tf_op jit(solution)/shard_map/ppermute | solution.py:298
  13.7 16.7 %collective-permute-start.3 = (s16[2,4,144,128]{3,2,1,0:T(8,128)(2,1)S(1)}, s16[2,4,144,128]{3,2,1,0:T(8,128)(2,1)S(1)}, u32[]{:S(2)}, u32[]{:S(2)}) collective-permute-start(s16[2,4,144,128]{3,2,1,0:T(8,128)(2,1)S(1)} %get-tuple-element.31), channel_id=1, source_target_pairs={{0,16},{8,24},{16,0},{24,8},{1,17},{9,25},{17,1},{25,9},{2,18},{10... | collective-permute-start | bytes 884744 | tf_op jit(solution)/shard_map/ppermute | solution.py:298
  15.2 15.2 %collective-permute-start.4 = (s16[2,4,144,128]{3,2,1,0:T(8,128)(2,1)S(1)}, s16[2,4,144,128]{3,2,1,0:T(8,128)(2,1)S(1)}, u32[]{:S(2)}, u32[]{:S(2)}) collective-permute-start(s16[2,4,144,128]{3,2,1,0:T(8,128)(2,1)S(1)} %get-tuple-element.32), channel_id=1, source_target_pairs={{0,24},{8,16},{16,8},{24,0},{1,25},{9,17},{17,9},{25,1},{2,26},{10... | collective-permute-start | bytes 884744 | tf_op jit(solution)/shard_map/ppermute | solution.py:298
  15.7 7.7 %collective-permute-start.11 = (s16[8,80,128]{2,1,0:T(8,128)(2,1)S(1)}, s16[8,80,128]{2,1,0:T(8,128)(2,1)S(1)}, u32[]{:S(2)}, u32[]{:S(2)}) collective-permute-start(s16[8,80,128]{2,1,0:T(8,128)(2,1)S(1)} %get-tuple-element.41), channel_id=1, source_target_pairs={{0,6},{1,7},{2,4},{3,5},{4,2},{5,3},{6,0},{7,1},{8,14},{9,15},{10,... | collective-permute-start | bytes 491528 | tf_op jit(solution)/shard_map/ppermute | solution.py:298
  23.0 5.3 %collective-permute-start.9 = (s16[8,80,128]{2,1,0:T(8,128)(2,1)S(1)}, s16[8,80,128]{2,1,0:T(8,128)(2,1)S(1)}, u32[]{:S(2)}, u32[]{:S(2)}) collective-permute-start(s16[8,80,128]{2,1,0:T(8,128)(2,1)S(1)} %get-tuple-element.39), channel_id=1, source_target_pairs={{0,2},{1,3},{2,0},{3,1},{4,6},{5,7},{6,4},{7,5},{8,10},{9,11},{10,... | collective-permute-start | bytes 491528 | tf_op jit(solution)/shard_map/ppermute | solution.py:298
  28.5 8.3 %collective-permute-start.12 = (s16[2,80,128]{2,1,0:T(8,128)(2,1)S(1)}, s16[2,80,128]{2,1,0:T(8,128)(2,1)S(1)}, u32[]{:S(2)}, u32[]{:S(2)}) collective-permute-start(s16[2,80,128]{2,1,0:T(8,128)(2,1)S(1)} %get-tuple-element.43), channel_id=1, source_target_pairs={{0,8},{8,0},{16,24},{24,16},{1,9},{9,1},{17,25},{25,17},{2,10},{10... | collective-permute-start | bytes 122888 | tf_op jit(solution)/shard_map/ppermute | solution.py:298
  30.9 10.9 %collective-permute-start.5 = (s16[2,144,128]{2,1,0:T(8,128)(2,1)S(1)}, s16[2,144,128]{2,1,0:T(8,128)(2,1)S(1)}, u32[]{:S(2)}, u32[]{:S(2)}) collective-permute-start(s16[2,144,128]{2,1,0:T(8,128)(2,1)S(1)} %get-tuple-element.34), channel_id=1, source_target_pairs={{0,2},{1,3},{2,0},{3,1},{4,6},{5,7},{6,4},{7,5},{8,10},{9,11},{10,... | collective-permute-start | bytes 221192 | tf_op jit(solution)/shard_map/ppermute | solution.py:298
  31.8 9.9 %collective-permute-start.6 = (s16[2,144,128]{2,1,0:T(8,128)(2,1)S(1)}, s16[2,144,128]{2,1,0:T(8,128)(2,1)S(1)}, u32[]{:S(2)}, u32[]{:S(2)}) collective-permute-start(s16[2,144,128]{2,1,0:T(8,128)(2,1)S(1)} %get-tuple-element.35), channel_id=1, source_target_pairs={{0,4},{1,5},{2,6},{3,7},{4,0},{5,1},{6,2},{7,3},{8,12},{9,13},{10,... | collective-permute-start | bytes 221192 | tf_op jit(solution)/shard_map/ppermute | solution.py:298
  35.2 6.5 %collective-permute-start.7 = (s16[2,144,128]{2,1,0:T(8,128)(2,1)S(1)}, s16[2,144,128]{2,1,0:T(8,128)(2,1)S(1)}, u32[]{:S(2)}, u32[]{:S(2)}) collective-permute-start(s16[2,144,128]{2,1,0:T(8,128)(2,1)S(1)} %get-tuple-element.36), channel_id=1, source_target_pairs={{0,6},{1,7},{2,4},{3,5},{4,2},{5,3},{6,0},{7,1},{8,14},{9,15},{10,... | collective-permute-start | bytes 221192 | tf_op jit(solution)/shard_map/ppermute | solution.py:298
  35.3 4.0 %collective-permute-start.13 = (s16[2,80,128]{2,1,0:T(8,128)(2,1)S(1)}, s16[2,80,128]{2,1,0:T(8,128)(2,1)S(1)}, u32[]{:S(2)}, u32[]{:S(2)}) collective-permute-start(s16[2,80,128]{2,1,0:T(8,128)(2,1)S(1)} %get-tuple-element.44), channel_id=1, source_target_pairs={{0,16},{8,24},{16,0},{24,8},{1,17},{9,25},{17,1},{25,9},{2,18},{10... | collective-permute-start | bytes 122888 | tf_op jit(solution)/shard_map/ppermute | solution.py:298
  36.8 4.9 %collective-permute-start.14 = (s16[2,80,128]{2,1,0:T(8,128)(2,1)S(1)}, s16[2,80,128]{2,1,0:T(8,128)(2,1)S(1)}, u32[]{:S(2)}, u32[]{:S(2)}) collective-permute-start(s16[2,80,128]{2,1,0:T(8,128)(2,1)S(1)} %get-tuple-element.45), channel_id=1, source_target_pairs={{0,24},{8,16},{16,8},{24,0},{1,25},{9,17},{17,9},{25,1},{2,26},{10... | collective-permute-start | bytes 122888 | tf_op jit(solution)/shard_map/ppermute | solution.py:298

commit v3 on v2

--- a/solution.py
+++ b/solution.py
@@ -183,7 +183,7 @@
 def finish(n_cls, n_z, cuts, wedges, weights, *refs):
     pos = position()
     sides = (refs[:n_z], refs[n_z : n_z + n_cls])
-    average, totals, scratch = refs[n_z + n_cls :]
+    out, out_totals, scratch, average, totals, sems = refs[n_z + n_cls :]
     stride = weights.shape[1] // wedges
     held, rows = average.shape[0], average.shape[1]
     shape = (up(wedges), LANES)
@@ -212,17 +212,26 @@
                 sums = ends[h][SUB:]
             scratch[h, low:high] = weight[h]
             average[h, low:high] = sums / (weight[h] + 1.0)
+        if low == 0:
+            first = pltpu.make_async_copy(average.at[:, :cut], out.at[:, :cut], sems.at[0])
+            first.start()
     for h in range(held):
         tiles = rows // PARTS
         totals[pl.ds(h, tiles, stride=held), :] = scratch[h, pl.ds(0, tiles, stride=PARTS), :]
-
-
-def call(body, operands, specs, shapes, scratch=(), flops=1 << 22, limit=16):
+    second = pltpu.make_async_copy(average.at[:, cut:rows], out.at[:, cut:rows], sems.at[1])
+    third = pltpu.make_async_copy(totals, out_totals, sems.at[2])
+    second.start()
+    third.start()
+    for copy in (first, second, third):
+        copy.wait()
+
+
+def call(body, operands, specs, shapes, scratch=(), flops=1 << 22, limit=16, places=None):
     return pl.pallas_call(
         body,
         out_shape=shapes,
         in_specs=specs,
-        out_specs=[VMEM] * len(shapes),
+        out_specs=places or [VMEM] * len(shapes),
         scratch_shapes=list(scratch),
         compiler_params=pltpu.CompilerParams(vmem_limit_bytes=limit * 1024 * 1024),
         cost_estimate=pl.CostEstimate(flops=flops, bytes_accessed=flops, transcendentals=0),
@@ -319,7 +328,13 @@
         (weights, *head, *ends),
         [VMEM] * (1 + n_z + n_cls),
         [array((CLS_GROUP, rows), jnp.float32), array((tiles * CLS_GROUP,), jnp.float32)],
-        scratch=[pltpu.VMEM((CLS_GROUP, rows, LANES), jnp.float32)],
+        scratch=[
+            pltpu.VMEM((CLS_GROUP, rows, LANES), jnp.float32),
+            pltpu.VMEM((CLS_GROUP, rows, LANES), jnp.float32),
+            pltpu.VMEM((tiles * CLS_GROUP, LANES), jnp.float32),
+            DMA((3,)),
+        ],
+        places=[HBM, HBM],
     )
     average = average.reshape(CLS_GROUP, tiles, parts, LANES).transpose(0, 2, 1, 3)
     average = with_layout_constraint(average, Layout(major_to_minor=(0, 2, 1, 3)))

time: 43 us -> 43 us (level)
  no operation moved by 1% of the time
where the time goes in v3:
time: 43 us; the launch traced here: 42.8 us
  starting transfers between devices  18.5 us (43%)
  waiting for transfers between devices  15.3 us (36%)
  Pallas kernels  8.29 us (19%)
  between operations  0.72 us (2%)
    ppermute x12, starting transfers between devices, over(): moved[i] = lax.ppermute(arrays[i], axis, moves[i])  17.4 us
    ppermute x12, waiting for transfers between devices, over(): moved[i] = lax.ppermute(arrays[i], axis, moves[i])  15.3 us
    pallas_call x7, Pallas kernels, call(): pl.pallas_call(body, out_shape=shapes, in_specs=specs, out_specs=places o...  8.29 us
  transfers between devices with their start and end apart: 15, of which 4 were waited for; matrix products, arithmetic and copies ran while one was open for 0% of the time, Pallas kernels for 13%

profile of v3, /device:TPU:0, one launch (start us, length us, event | category | flops | bytes accessed | tf_op | source)
XLA Modules:
  0.0 42.8 jit_solution(8932573950539744996)
XLA Ops:
  0.6 1.5 %shard_map.60 = (bf16[8,4,144,128]{3,2,1,0:T(8,128)(2,1)S(1)}, bf16[8,4,80,128]{3,2,1,0:T(8,128)(2,1)S(1)}) custom-call(bf16[8,8,216,128]{3,2,1,0:T(8,128)(2,1)} %bitcast.17), custom_call_target="tpu_custom_call" | custom-call | flops 4194304 | bytes 4194304 | tf_op jit(solution)/shard_map/pallas_call | solution.py:230
  2.2 0.6 %collective-permute-start.1 = (bf16[8,4,144,128]{3,2,1,0:T(8,128)(2,1)S(1)}, bf16[8,4,144,128]{3,2,1,0:T(8,128)(2,1)S(1)}, u32[]{:S(2)}, u32[]{:S(2)}) collective-permute-start(bf16[8,4,144,128]{3,2,1,0:T(8,128)(2,1)S(1)} %get-tuple-element.26), channel_id=1, source_target_pairs={{0,1},{1,0},{2,3},{3,2},{4,5},{5,4},{6,7},{7,6},{8,9},{9,8},{10,11... | collective-permute-start | bytes 3538952 | tf_op jit(solution)/shard_map/ppermute | solution.py:277
  2.7 0.1 collective-permute-start.8
  2.8 0.5 %collective-permute-start = (s32[2,8]{1,0:T(2,128)S(1)}, s32[2,8]{1,0:T(2,128)S(1)}, u32[]{:S(2)}, u32[]{:S(2)}) collective-permute-start(s32[2,8]{1,0:T(2,128)S(1)} %pad_add_fusion.meta), channel_id=1, source_target_pairs={{0,1},{1,0},{2,3},{3,2},{4,5},{5,4},{6,7},{7,6},{8,9},{9,8},{10,11... | collective-permute-start | bytes 200 | tf_op jit(solution)/shard_map/ppermute | solution.py:276
  3.3 3.0 %shard_map.59 = (f32[4,2592,128]{2,1,0:T(8,128)S(1)}, f32[8,4,216,128]{3,2,1,0:T(8,128)S(1)}, f32[8,8,128]{2,1,0:T(8,128)S(1)}) custom-call(s32[2,8]{1,0:T(2,128)S(1)} %pad_add_fusion.meta, f32[12,110592]{1,0:T(8,128)} %table.1, bf16[8,8,216,128]{3,2,1,0:T(8,128)(2,1)} %bitcast.18), custom_call_target="tpu_custom_call" | custom-call | flops 16777216 | bytes 16777216 | tf_op jit(solution)/shard_map/pallas_call | solution.py:230
  6.3 0.0 collective-permute-done.got_meta
  6.3 0.0 collective-permute-done.8.got
  6.3 0.7 %shard_map.63 = (s16[8,80,128]{2,1,0:T(8,128)(2,1)S(1)}, s16[8,80,128]{2,1,0:T(8,128)(2,1)S(1)}, s16[8,80,128]{2,1,0:T(8,128)(2,1)S(1)}, s16[8,80,128]{2,1,0:T(8,128)(2,1)S(1)}) custom-call(s32[2,8]{1,0:T(2,128)S(1)} %collective-permute-done.got_meta, bf16[8,4,80,128]{3,2,1,0:T(8,128)(2,1)S(1)} %collective-permute-done.8.got, ...), custom_call_target="tpu_custom_call" | custom-call | flops 4194304 | bytes 4194304 | tf_op jit(solution)/shard_map/pallas_call | solution.py:230
  7.1 3.8 %collective-permute-start.10 = (s16[8,80,128]{2,1,0:T(8,128)(2,1)S(1)}, s16[8,80,128]{2,1,0:T(8,128)(2,1)S(1)}, u32[]{:S(2)}, u32[]{:S(2)}) collective-permute-start(s16[8,80,128]{2,1,0:T(8,128)(2,1)S(1)} %get-tuple-element.40), channel_id=1, source_target_pairs={{0,4},{1,5},{2,6},{3,7},{4,0},{5,1},{6,2},{7,3},{8,12},{9,13},{10,... | collective-permute-start | bytes 491528 | tf_op jit(solution)/shard_map/ppermute | solution.py:307
  10.9 1.2 %shard_map.61 = (s16[2,4,144,128]{3,2,1,0:T(8,128)(2,1)S(1)}, s16[2,4,144,128]{3,2,1,0:T(8,128)(2,1)S(1)}, s16[2,4,144,128]{3,2,1,0:T(8,128)(2,1)S(1)}, s16[2,4,144,128]{3,2,1,0:T(8,128)(2,1)S(1)}) custom-call(s32[2,8]{1,0:T(2,128)S(1)} %collective-permute-done.got_meta, bf16[8,4,144,128]{3,2,1,0:T(8,128)(2,1)S(1)} %collective-permute-done.1.got, ...), custom_call_target="tpu_custom_call" | custom-call | flops 4194304 | bytes 4194304 | tf_op jit(solution)/shard_map/pallas_call | solution.py:230
  12.1 1.6 %collective-permute-start.2 = (s16[2,4,144,128]{3,2,1,0:T(8,128)(2,1)S(1)}, s16[2,4,144,128]{3,2,1,0:T(8,128)(2,1)S(1)}, u32[]{:S(2)}, u32[]{:S(2)}) collective-permute-start(s16[2,4,144,128]{3,2,1,0:T(8,128)(2,1)S(1)} %get-tuple-element.30), channel_id=1, source_target_pairs={{0,8},{8,0},{16,24},{24,16},{1,9},{9,1},{17,25},{25,17},{2,10},{10... | collective-permute-start | bytes 884744 | tf_op jit(solution)/shard_map/ppermute | solution.py:307
  13.7 1.5 %collective-permute-start.3 = (s16[2,4,144,128]{3,2,1,0:T(8,128)(2,1)S(1)}, s16[2,4,144,128]{3,2,1,0:T(8,128)(2,1)S(1)}, u32[]{:S(2)}, u32[]{:S(2)}) collective-permute-start(s16[2,4,144,128]{3,2,1,0:T(8,128)(2,1)S(1)} %get-tuple-element.31), channel_id=1, source_target_pairs={{0,16},{8,24},{16,0},{24,8},{1,17},{9,25},{17,1},{25,9},{2,18},{10... | collective-permute-start | bytes 884744 | tf_op jit(solution)/shard_map/ppermute | solution.py:307
  15.2 0.5 %collective-permute-start.4 = (s16[2,4,144,128]{3,2,1,0:T(8,128)(2,1)S(1)}, s16[2,4,144,128]{3,2,1,0:T(8,128)(2,1)S(1)}, u32[]{:S(2)}, u32[]{:S(2)}) collective-permute-start(s16[2,4,144,128]{3,2,1,0:T(8,128)(2,1)S(1)} %get-tuple-element.32), channel_id=1, source_target_pairs={{0,24},{8,16},{16,8},{24,0},{1,25},{9,17},{17,9},{25,1},{2,26},{10... | collective-permute-start | bytes 884744 | tf_op jit(solution)/shard_map/ppermute | solution.py:307
  15.7 1.4 %collective-permute-start.11 = (s16[8,80,128]{2,1,0:T(8,128)(2,1)S(1)}, s16[8,80,128]{2,1,0:T(8,128)(2,1)S(1)}, u32[]{:S(2)}, u32[]{:S(2)}) collective-permute-start(s16[8,80,128]{2,1,0:T(8,128)(2,1)S(1)} %get-tuple-element.41), channel_id=1, source_target_pairs={{0,6},{1,7},{2,4},{3,5},{4,2},{5,3},{6,0},{7,1},{8,14},{9,15},{10,... | collective-permute-start | bytes 491528 | tf_op jit(solution)/shard_map/ppermute | solution.py:307
  17.1 5.9 %collective-permute-done.10.refs_2_ = s16[8,80,128]{2,1,0:T(8,128)(2,1)S(1)} collective-permute-done((s16[8,80,128]{2,1,0:T(8,128)(2,1)S(1)}, s16[8,80,128]{2,1,0:T(8,128)(2,1)S(1)}, u32[]{:S(2)}, u32[]{:S(2)}) %collective-permute-start.10) | collective-permute-done | bytes 163872 | tf_op jit(solution)/shard_map/ppermute | solution.py:307
  23.0 0.4 %collective-permute-start.9 = (s16[8,80,128]{2,1,0:T(8,128)(2,1)S(1)}, s16[8,80,128]{2,1,0:T(8,128)(2,1)S(1)}, u32[]{:S(2)}, u32[]{:S(2)}) collective-permute-start(s16[8,80,128]{2,1,0:T(8,128)(2,1)S(1)} %get-tuple-element.39), channel_id=1, source_target_pairs={{0,2},{1,3},{2,0},{3,1},{4,6},{5,7},{6,4},{7,5},{8,10},{9,11},{10,... | collective-permute-start | bytes 491528 | tf_op jit(solution)/shard_map/ppermute | solution.py:307
  23.4 0.0 collective-permute-done.11.refs_3_
  23.4 4.9 %collective-permute-done.9.refs_1_ = s16[8,80,128]{2,1,0:T(8,128)(2,1)S(1)} collective-permute-done((s16[8,80,128]{2,1,0:T(8,128)(2,1)S(1)}, s16[8,80,128]{2,1,0:T(8,128)(2,1)S(1)}, u32[]{:S(2)}, u32[]{:S(2)}) %collective-permute-start.9) | collective-permute-done | bytes 163872 | tf_op jit(solution)/shard_map/ppermute | solution.py:307
  28.3 0.3 shard_map.64
  28.5 1.9 %collective-permute-start.12 = (s16[2,80,128]{2,1,0:T(8,128)(2,1)S(1)}, s16[2,80,128]{2,1,0:T(8,128)(2,1)S(1)}, u32[]{:S(2)}, u32[]{:S(2)}) collective-permute-start(s16[2,80,128]{2,1,0:T(8,128)(2,1)S(1)} %get-tuple-element.43), channel_id=1, source_target_pairs={{0,8},{8,0},{16,24},{24,16},{1,9},{9,1},{17,25},{25,17},{2,10},{10... | collective-permute-start | bytes 122888 | tf_op jit(solution)/shard_map/ppermute | solution.py:307
  30.4 0.0 collective-permute-done.2.refs_1_
  30.4 0.0 collective-permute-done.3.refs_2_
  30.4 0.0 collective-permute-done.4.refs_3_
  30.4 0.4 %shard_map.62 = (s16[2,144,128]{2,1,0:T(8,128)(2,1)S(1)}, s16[2,144,128]{2,1,0:T(8,128)(2,1)S(1)}, s16[2,144,128]{2,1,0:T(8,128)(2,1)S(1)}, s16[2,144,128]{2,1,0:T(8,128)(2,1)S(1)}) custom-call(s16[2,4,144,128]{3,2,1,0:T(8,128)(2,1)S(1)} %get-tuple-element.29.refs_0_, s16[2,4,144,128]{3,2,1,0:T(8,128)(2,1)S(1)} %collective-permute-done.2.refs_1_, ...), custom_call_target="tpu_custom_call" | custom-call | flops 4194304 | bytes 4194304 | tf_op jit(solution)/shard_map/pallas_call | solution.py:230
  30.9 1.0 %collective-permute-start.5 = (s16[2,144,128]{2,1,0:T(8,128)(2,1)S(1)}, s16[2,144,128]{2,1,0:T(8,128)(2,1)S(1)}, u32[]{:S(2)}, u32[]{:S(2)}) collective-permute-start(s16[2,144,128]{2,1,0:T(8,128)(2,1)S(1)} %get-tuple-element.34), channel_id=1, source_target_pairs={{0,2},{1,3},{2,0},{3,1},{4,6},{5,7},{6,4},{7,5},{8,10},{9,11},{10,... | collective-permute-start | bytes 221192 | tf_op jit(solution)/shard_map/ppermute | solution.py:307
  31.8 3.4 %collective-permute-start.6 = (s16[2,144,128]{2,1,0:T(8,128)(2,1)S(1)}, s16[2,144,128]{2,1,0:T(8,128)(2,1)S(1)}, u32[]{:S(2)}, u32[]{:S(2)}) collective-permute-start(s16[2,144,128]{2,1,0:T(8,128)(2,1)S(1)} %get-tuple-element.35), channel_id=1, source_target_pairs={{0,4},{1,5},{2,6},{3,7},{4,0},{5,1},{6,2},{7,3},{8,12},{9,13},{10,... | collective-permute-start | bytes 221192 | tf_op jit(solution)/shard_map/ppermute | solution.py:307
  35.2 0.1 collective-permute-start.7
  35.3 1.5 %collective-permute-start.13 = (s16[2,80,128]{2,1,0:T(8,128)(2,1)S(1)}, s16[2,80,128]{2,1,0:T(8,128)(2,1)S(1)}, u32[]{:S(2)}, u32[]{:S(2)}) collective-permute-start(s16[2,80,128]{2,1,0:T(8,128)(2,1)S(1)} %get-tuple-element.44), channel_id=1, source_target_pairs={{0,16},{8,24},{16,0},{24,8},{1,17},{9,25},{17,1},{25,9},{2,18},{10... | collective-permute-start | bytes 122888 | tf_op jit(solution)/shard_map/ppermute | solution.py:307
  36.8 0.4 collective-permute-start.14
  37.2 2.1 %collective-permute-done.13.refs_6_ = s16[2,80,128]{2,1,0:T(8,128)(2,1)S(1)} collective-permute-done((s16[2,80,128]{2,1,0:T(8,128)(2,1)S(1)}, s16[2,80,128]{2,1,0:T(8,128)(2,1)S(1)}, u32[]{:S(2)}, u32[]{:S(2)}) %collective-permute-start.13) | collective-permute-done | bytes 40992 | tf_op jit(solution)/shard_map/ppermute | solution.py:307
  39.3 2.4 %collective-permute-done.14.refs_7_ = s16[2,80,128]{2,1,0:T(8,128)(2,1)S(1)} collective-permute-done((s16[2,80,128]{2,1,0:T(8,128)(2,1)S(1)}, s16[2,80,128]{2,1,0:T(8,128)(2,1)S(1)}, u32[]{:S(2)}, u32[]{:S(2)}) %collective-permute-start.14) | collective-permute-done | bytes 40992 | tf_op jit(solution)/shard_map/ppermute | solution.py:307
  41.7 1.1 %shard_map.65 = (f32[2,216,128]{2,1,0:T(8,128)}, f32[216,128]{1,0:T(8,128)}) custom-call(f32[4,2592,128]{2,1,0:T(8,128)S(1)} %get-tuple-element.25.weights, s16[2,144,128]{2,1,0:T(8,128)(2,1)S(1)} %get-tuple-element.33.refs_0_, s16[2,144,128]{2,1,0:T(8,128)(2,1)S(1)} %collective-permute-done.5.refs_1_, ...), custom_call_target="tpu_custom_call" | custom-call | flops 4194304 | bytes 4194304 | tf_op jit(solution)/shard_map/pallas_call | solution.py:230
  (10 shorter events, 0.0 us)
Async XLA Ops:
  0.6 2.2 %copy-start.1 = (s32[8,1]{0,1:T(1,128)S(1)}, s32[8,1]{0,1:T(1,128)}, u32[]{:S(2)}) copy-start(s32[8,1]{0,1:T(1,128)} %param.5) | copy-start | bytes 100
  0.6 2.2 %copy-start = (s32[8]{0:T(128)S(1)}, s32[8]{0:T(128)}, u32[]{:S(2)}) copy-start(s32[8]{0:T(128)} %param.6) | copy-start | bytes 100
  2.2 8.7 %collective-permute-start.1 = (bf16[8,4,144,128]{3,2,1,0:T(8,128)(2,1)S(1)}, bf16[8,4,144,128]{3,2,1,0:T(8,128)(2,1)S(1)}, u32[]{:S(2)}, u32[]{:S(2)}) collective-permute-start(bf16[8,4,144,128]{3,2,1,0:T(8,128)(2,1)S(1)} %get-tuple-element.26), channel_id=1, source_target_pairs={{0,1},{1,0},{2,3},{3,2},{4,5},{5,4},{6,7},{7,6},{8,9},{9,8},{10,11... | collective-permute-start | bytes 3538952 | tf_op jit(solution)/shard_map/ppermute | solution.py:277
  2.7 3.6 %collective-permute-start.8 = (bf16[8,4,80,128]{3,2,1,0:T(8,128)(2,1)S(1)}, bf16[8,4,80,128]{3,2,1,0:T(8,128)(2,1)S(1)}, u32[]{:S(2)}, u32[]{:S(2)}) collective-permute-start(bf16[8,4,80,128]{3,2,1,0:T(8,128)(2,1)S(1)} %get-tuple-element.37), channel_id=1, source_target_pairs={{0,1},{1,0},{2,3},{3,2},{4,5},{5,4},{6,7},{7,6},{8,9},{9,8},{10,11... | collective-permute-start | bytes 1966088 | tf_op jit(solution)/shard_map/ppermute | solution.py:277
  2.8 3.5 %collective-permute-start = (s32[2,8]{1,0:T(2,128)S(1)}, s32[2,8]{1,0:T(2,128)S(1)}, u32[]{:S(2)}, u32[]{:S(2)}) collective-permute-start(s32[2,8]{1,0:T(2,128)S(1)} %pad_add_fusion.meta), channel_id=1, source_target_pairs={{0,1},{1,0},{2,3},{3,2},{4,5},{5,4},{6,7},{7,6},{8,9},{9,8},{10,11... | collective-permute-start | bytes 200 | tf_op jit(solution)/shard_map/ppermute | solution.py:276
  7.1 15.9 %collective-permute-start.10 = (s16[8,80,128]{2,1,0:T(8,128)(2,1)S(1)}, s16[8,80,128]{2,1,0:T(8,128)(2,1)S(1)}, u32[]{:S(2)}, u32[]{:S(2)}) collective-permute-start(s16[8,80,128]{2,1,0:T(8,128)(2,1)S(1)} %get-tuple-element.40), channel_id=1, source_target_pairs={{0,4},{1,5},{2,6},{3,7},{4,0},{5,1},{6,2},{7,3},{8,12},{9,13},{10,... | collective-permute-start | bytes 491528 | tf_op jit(solution)/shard_map/ppermute | solution.py:307
  12.1 18.3 %collective-permute-start.2 = (s16[2,4,144,128]{3,2,1,0:T(8,128)(2,1)S(1)}, s16[2,4,144,128]{3,2,1,0:T(8,128)(2,1)S(1)}, u32[]{:S(2)}, u32[]{:S(2)}) collective-permute-start(s16[2,4,144,128]{3,2,1,0:T(8,128)(2,1)S(1)} %get-tuple-element.30), channel_id=1, source_target_pairs={{0,8},{8,0},{16,24},{24,16},{1,9},{9,1},{17,25},{25,17},{2,10},{10... | collective-permute-start | bytes 884744 | tf_op jit(solution)/shard_map/ppermute | solution.py:307
  13.7 16.7 %collective-permute-start.3 = (s16[2,4,144,128]{3,2,1,0:T(8,128)(2,1)S(1)}, s16[2,4,144,128]{3,2,1,0:T(8,128)(2,1)S(1)}, u32[]{:S(2)}, u32[]{:S(2)}) collective-permute-start(s16[2,4,144,128]{3,2,1,0:T(8,128)(2,1)S(1)} %get-tuple-element.31), channel_id=1, source_target_pairs={{0,16},{8,24},{16,0},{24,8},{1,17},{9,25},{17,1},{25,9},{2,18},{10... | collective-permute-start | bytes 884744 | tf_op jit(solution)/shard_map/ppermute | solution.py:307
  15.2 15.2 %collective-permute-start.4 = (s16[2,4,144,128]{3,2,1,0:T(8,128)(2,1)S(1)}, s16[2,4,144,128]{3,2,1,0:T(8,128)(2,1)S(1)}, u32[]{:S(2)}, u32[]{:S(2)}) collective-permute-start(s16[2,4,144,128]{3,2,1,0:T(8,128)(2,1)S(1)} %get-tuple-element.32), channel_id=1, source_target_pairs={{0,24},{8,16},{16,8},{24,0},{1,25},{9,17},{17,9},{25,1},{2,26},{10... | collective-permute-start | bytes 884744 | tf_op jit(solution)/shard_map/ppermute | solution.py:307
  15.7 7.7 %collective-permute-start.11 = (s16[8,80,128]{2,1,0:T(8,128)(2,1)S(1)}, s16[8,80,128]{2,1,0:T(8,128)(2,1)S(1)}, u32[]{:S(2)}, u32[]{:S(2)}) collective-permute-start(s16[8,80,128]{2,1,0:T(8,128)(2,1)S(1)} %get-tuple-element.41), channel_id=1, source_target_pairs={{0,6},{1,7},{2,4},{3,5},{4,2},{5,3},{6,0},{7,1},{8,14},{9,15},{10,... | collective-permute-start | bytes 491528 | tf_op jit(solution)/shard_map/ppermute | solution.py:307
  23.0 5.3 %collective-permute-start.9 = (s16[8,80,128]{2,1,0:T(8,128)(2,1)S(1)}, s16[8,80,128]{2,1,0:T(8,128)(2,1)S(1)}, u32[]{:S(2)}, u32[]{:S(2)}) collective-permute-start(s16[8,80,128]{2,1,0:T(8,128)(2,1)S(1)} %get-tuple-element.39), channel_id=1, source_target_pairs={{0,2},{1,3},{2,0},{3,1},{4,6},{5,7},{6,4},{7,5},{8,10},{9,11},{10,... | collective-permute-start | bytes 491528 | tf_op jit(solution)/shard_map/ppermute | solution.py:307
  28.5 8.3 %collective-permute-start.12 = (s16[2,80,128]{2,1,0:T(8,128)(2,1)S(1)}, s16[2,80,128]{2,1,0:T(8,128)(2,1)S(1)}, u32[]{:S(2)}, u32[]{:S(2)}) collective-permute-start(s16[2,80,128]{2,1,0:T(8,128)(2,1)S(1)} %get-tuple-element.43), channel_id=1, source_target_pairs={{0,8},{8,0},{16,24},{24,16},{1,9},{9,1},{17,25},{25,17},{2,10},{10... | collective-permute-start | bytes 122888 | tf_op jit(solution)/shard_map/ppermute | solution.py:307
  30.9 10.9 %collective-permute-start.5 = (s16[2,144,128]{2,1,0:T(8,128)(2,1)S(1)}, s16[2,144,128]{2,1,0:T(8,128)(2,1)S(1)}, u32[]{:S(2)}, u32[]{:S(2)}) collective-permute-start(s16[2,144,128]{2,1,0:T(8,128)(2,1)S(1)} %get-tuple-element.34), channel_id=1, source_target_pairs={{0,2},{1,3},{2,0},{3,1},{4,6},{5,7},{6,4},{7,5},{8,10},{9,11},{10,... | collective-permute-start | bytes 221192 | tf_op jit(solution)/shard_map/ppermute | solution.py:307
  31.8 9.9 %collective-permute-start.6 = (s16[2,144,128]{2,1,0:T(8,128)(2,1)S(1)}, s16[2,144,128]{2,1,0:T(8,128)(2,1)S(1)}, u32[]{:S(2)}, u32[]{:S(2)}) collective-permute-start(s16[2,144,128]{2,1,0:T(8,128)(2,1)S(1)} %get-tuple-element.35), channel_id=1, source_target_pairs={{0,4},{1,5},{2,6},{3,7},{4,0},{5,1},{6,2},{7,3},{8,12},{9,13},{10,... | collective-permute-start | bytes 221192 | tf_op jit(solution)/shard_map/ppermute | solution.py:307
  35.2 6.5 %collective-permute-start.7 = (s16[2,144,128]{2,1,0:T(8,128)(2,1)S(1)}, s16[2,144,128]{2,1,0:T(8,128)(2,1)S(1)}, u32[]{:S(2)}, u32[]{:S(2)}) collective-permute-start(s16[2,144,128]{2,1,0:T(8,128)(2,1)S(1)} %get-tuple-element.36), channel_id=1, source_target_pairs={{0,6},{1,7},{2,4},{3,5},{4,2},{5,3},{6,0},{7,1},{8,14},{9,15},{10,... | collective-permute-start | bytes 221192 | tf_op jit(solution)/shard_map/ppermute | solution.py:307
  35.3 4.0 %collective-permute-start.13 = (s16[2,80,128]{2,1,0:T(8,128)(2,1)S(1)}, s16[2,80,128]{2,1,0:T(8,128)(2,1)S(1)}, u32[]{:S(2)}, u32[]{:S(2)}) collective-permute-start(s16[2,80,128]{2,1,0:T(8,128)(2,1)S(1)} %get-tuple-element.44), channel_id=1, source_target_pairs={{0,16},{8,24},{16,0},{24,8},{1,17},{9,25},{17,1},{25,9},{2,18},{10... | collective-permute-start | bytes 122888 | tf_op jit(solution)/shard_map/ppermute | solution.py:307
  36.8 4.9 %collective-permute-start.14 = (s16[2,80,128]{2,1,0:T(8,128)(2,1)S(1)}, s16[2,80,128]{2,1,0:T(8,128)(2,1)S(1)}, u32[]{:S(2)}, u32[]{:S(2)}) collective-permute-start(s16[2,80,128]{2,1,0:T(8,128)(2,1)S(1)} %get-tuple-element.45), channel_id=1, source_target_pairs={{0,24},{8,16},{16,8},{24,0},{1,25},{9,17},{17,9},{25,1},{2,26},{10... | collective-permute-start | bytes 122888 | tf_op jit(solution)/shard_map/ppermute | solution.py:307
